TPU v7x, 32 devices: a whole 2x2x4 slice. The times are simulated.
32 devices in a mesh: dp: 2 (over x), cp: 16 (over z, y, core).
Axes of the slice: x: 2, y: 2, z: 4, core: 2. Of those that a mesh axis runs over, the one named last changes fastest.
Arguments:
- image: bfloat16 [2, 6144, 3072], P('dp', 'cp'), parts along dimension 0
- text: bfloat16 [2, 256, 3072], P('dp'), parts along dimension 0
- cond_vec: bfloat16 [2, 3072], P('dp'), parts along dimension 0
- image_ids: int32 [12288, 3], P(('dp', 'cp')), parts along dimension 0
- img_w_mod: bfloat16 [3072, 18432], replicated
- img_b_mod: bfloat16 [18432], replicated
- img_w_qkv: bfloat16 [3072, 9216], replicated
- img_b_qkv: bfloat16 [9216], replicated
- img_q_gain: bfloat16 [128], replicated
- img_k_gain: bfloat16 [128], replicated
- img_w_proj: bfloat16 [3072, 3072], replicated
- img_b_proj: bfloat16 [3072], replicated
- img_w_fc1: bfloat16 [3072, 12288], replicated
- img_b_fc1: bfloat16 [12288], replicated
- img_w_fc2: bfloat16 [12288, 3072], replicated
- img_b_fc2: bfloat16 [3072], replicated
- txt_w_mod: bfloat16 [3072, 18432], replicated
- txt_b_mod: bfloat16 [18432], replicated
- txt_w_qkv: bfloat16 [3072, 9216], replicated
- txt_b_qkv: bfloat16 [9216], replicated
- txt_q_gain: bfloat16 [128], replicated
- txt_k_gain: bfloat16 [128], replicated
- txt_w_proj: bfloat16 [3072, 3072], replicated
- txt_b_proj: bfloat16 [3072], replicated
- txt_w_fc1: bfloat16 [3072, 12288], replicated
- txt_b_fc1: bfloat16 [12288], replicated
- txt_w_fc2: bfloat16 [12288, 3072], replicated
- txt_b_fc2: bfloat16 [3072], replicated
Outputs:
- output 1: bfloat16 [2, 6144, 3072], P('dp', 'cp'), parts along dimension 0
- output 2: bfloat16 [2, 256, 3072], P('dp'), parts along dimension 0
There are 2 independent parts. A program takes and returns all parts, laid end to end along the dimension named above; an argument that names none is the same for every part.
All inputs are finite; a program needn't handle non-finite values.
Results may differ from a plain program's by a relative error of at most 0.00561117.
Values are sent between devices in bfloat16 or wider.
A program may use at most 2.75 GiB of HBM per device.

v0:
```python
import jax
import jax.numpy as jnp
from jax import lax
from jax.sharding import PartitionSpec as P

EPS = 1e-6
THETA = 10000.0


def layer_norm(x):
    mean_x = jnp.mean(x, axis=-1, keepdims=True)
    centered = x - mean_x
    var_x = jnp.mean(centered * centered, axis=-1, keepdims=True)
    return centered * lax.rsqrt(var_x + EPS)


def head_norm(x, gain):
    mean_sq = jnp.mean(x * x, axis=-1, keepdims=True)
    return x * lax.rsqrt(mean_sq + EPS) * gain.astype(jnp.float32)


def rope_angles(pos_ids, head_size):
    rope_t = head_size // 8
    rope_s = (head_size - rope_t) // 2
    positions = pos_ids.astype(jnp.float32)
    pieces = []
    for axis_idx, width in enumerate((rope_t, rope_s, rope_s)):
        omega = THETA ** (-jnp.arange(0, width, 2, dtype=jnp.float32) / width)
        pieces.append(positions[:, axis_idx:axis_idx + 1] * omega[None, :])
    return jnp.concatenate(pieces, axis=-1)


def apply_rope(x, cos_a, sin_a):
    pairs = x.reshape(x.shape[:-1] + (x.shape[-1] // 2, 2))
    even = pairs[..., 0]
    odd = pairs[..., 1]
    turned = jnp.stack([cos_a * even - sin_a * odd, sin_a * even + cos_a * odd], axis=-1)
    return turned.reshape(x.shape)


def modulation(cond_act, w_mod, b_mod):
    mod_all = jnp.dot(cond_act, w_mod, preferred_element_type=jnp.float32) + b_mod.astype(jnp.float32)
    return jnp.split(mod_all[:, None, :], 6, axis=-1)


def branch_qkv(x, mod_rows, w_qkv, b_qkv, q_gain, k_gain):
    head_size = q_gain.shape[0]
    normed = ((1.0 + mod_rows[1]) * layer_norm(x.astype(jnp.float32)) + mod_rows[0]).astype(jnp.bfloat16)
    qkv_proj = jnp.dot(normed, w_qkv, preferred_element_type=jnp.float32) + b_qkv.astype(jnp.float32)
    batch, length, width = qkv_proj.shape
    qkv_proj = qkv_proj.reshape(batch, length, 3, width // (3 * head_size), head_size)
    query = head_norm(qkv_proj[:, :, 0], q_gain)
    keys = head_norm(qkv_proj[:, :, 1], k_gain)
    values = qkv_proj[:, :, 2].astype(jnp.bfloat16)
    return query, keys, values


def branch_out(x, attn_part, mod_rows, w_proj, b_proj, w_fc1, b_fc1, w_fc2, b_fc2):
    proj_out = jnp.dot(attn_part, w_proj, preferred_element_type=jnp.float32) + b_proj.astype(jnp.float32)
    resid_mid = x.astype(jnp.float32) + mod_rows[2] * proj_out
    normed = ((1.0 + mod_rows[4]) * layer_norm(resid_mid) + mod_rows[3]).astype(jnp.bfloat16)
    hidden = jnp.dot(normed, w_fc1, preferred_element_type=jnp.float32) + b_fc1.astype(jnp.float32)
    hidden = jax.nn.gelu(hidden, approximate=True).astype(jnp.bfloat16)
    mlp_out = jnp.dot(hidden, w_fc2, preferred_element_type=jnp.float32) + b_fc2.astype(jnp.float32)
    return (resid_mid + mod_rows[5] * mlp_out).astype(jnp.bfloat16)


def partial_attend(queries, keys_all, vals_all):
    scale = queries.shape[-1] ** -0.5
    scores = jnp.einsum('bqhd,bkhd->bhqk', queries, keys_all, preferred_element_type=jnp.float32) * scale
    peak = jnp.max(scores, axis=-1)
    exp_w = jnp.exp(scores - peak[..., None])
    total = jnp.sum(exp_w, axis=-1)
    acc_out = jnp.einsum('bhqk,bkhd->bqhd', exp_w.astype(jnp.bfloat16), vals_all, preferred_element_type=jnp.float32)
    return peak, total, acc_out


def attend(queries, keys_all, vals_all):
    stats = partial_attend(queries, keys_all, vals_all)
    out_heads = stats[2] / jnp.swapaxes(stats[1], 1, 2)[..., None]
    return out_heads.astype(jnp.bfloat16).reshape(queries.shape[0], queries.shape[1], -1)


def text_attend(txt_q, txt_k, txt_v, img_k, img_v):
    head_size = txt_q.shape[-1]
    img_peak, img_total, img_acc = partial_attend(txt_q, img_k, img_v)
    peak_all = lax.pmax(img_peak, 'cp')
    factor = jnp.swapaxes(jnp.exp(img_peak - peak_all), 1, 2)[..., None]
    packed = jnp.concatenate([img_acc * factor, jnp.swapaxes(img_total, 1, 2)[..., None] * factor], axis=-1)
    packed = lax.psum(packed, 'cp')
    self_peak, self_total, self_acc = partial_attend(txt_q, txt_k, txt_v)
    peak_fin = jnp.maximum(peak_all, self_peak)
    img_scale = jnp.swapaxes(jnp.exp(peak_all - peak_fin), 1, 2)[..., None]
    self_scale = jnp.swapaxes(jnp.exp(self_peak - peak_fin), 1, 2)[..., None]
    acc_fin = packed[..., :head_size] * img_scale + self_acc * self_scale
    total_fin = packed[..., head_size:] * img_scale + jnp.swapaxes(self_total, 1, 2)[..., None] * self_scale
    return (acc_fin / total_fin).astype(jnp.bfloat16).reshape(txt_q.shape[0], txt_q.shape[1], -1)


def solution(mesh):
    act_spec = P('dp', 'cp', None)
    text_spec = P('dp', None, None)
    in_specs = (act_spec, text_spec, P('dp', None), P(('dp', 'cp'), None)) + (P(),) * 24
    out_specs = (act_spec, text_spec)

    def device_fn(image, text, cond_vec, image_ids, *weights):
        img_w = weights[:12]
        txt_w = weights[12:]
        head_size = img_w[4].shape[0]
        cond_act = jax.nn.silu(cond_vec.astype(jnp.float32)).astype(jnp.bfloat16)
        img_mods = modulation(cond_act, img_w[0], img_w[1])
        txt_mods = modulation(cond_act, txt_w[0], txt_w[1])
        img_q, img_k, img_v = branch_qkv(image, img_mods, img_w[2], img_w[3], img_w[4], img_w[5])
        txt_q, txt_k, txt_v = branch_qkv(text, txt_mods, txt_w[2], txt_w[3], txt_w[4], txt_w[5])
        angles = rope_angles(image_ids, head_size)[None, :, None, :]
        cos_a = jnp.cos(angles)
        sin_a = jnp.sin(angles)
        img_q = apply_rope(img_q, cos_a, sin_a).astype(jnp.bfloat16)
        img_k = apply_rope(img_k, cos_a, sin_a).astype(jnp.bfloat16)
        txt_q = txt_q.astype(jnp.bfloat16)
        txt_k = txt_k.astype(jnp.bfloat16)
        img_k_all = lax.all_gather(img_k, 'cp', axis=1, tiled=True)
        img_v_all = lax.all_gather(img_v, 'cp', axis=1, tiled=True)
        keys_all = jnp.concatenate([txt_k, img_k_all], axis=1)
        vals_all = jnp.concatenate([txt_v, img_v_all], axis=1)
        img_attn = attend(img_q, keys_all, vals_all)
        txt_attn = text_attend(txt_q, txt_k, txt_v, img_k, img_v)
        image_out = branch_out(image, img_attn, img_mods, img_w[6], img_w[7], img_w[8], img_w[9], img_w[10], img_w[11])
        text_out = branch_out(text, txt_attn, txt_mods, txt_w[6], txt_w[7], txt_w[8], txt_w[9], txt_w[10], txt_w[11])
        return image_out, text_out

    return jax.shard_map(device_fn, mesh=mesh, in_specs=in_specs, out_specs=out_specs, check_vma=False)
```

profile of v0, /device:TPU:0, one launch (start us, length us, event | category | flops | bytes accessed | tf_op | source)
XLA Modules:
  0.0 947.9 jit_solution(9977627732808139430)
XLA Ops:
  8.3 37.2 %fusion.148 = f32[1,18432]{1,0:T(1,128)S(1)} fusion(bf16[3072,18432]{1,0:T(8,128)(2,1)} %param.32, bf16[1,3072]{1,0:T(2,128)(2,1)} %param.30), kind=kOutput, calls=%fused_computation.188 | convolution fusion | flops 113264640 | bytes 113326080 | tf_op jit(solution)/shard_map/dot_general | solution.py:42
  47.4 31.7 %add_bitcast_fusion = f32[48,8,72,128]{3,1,2,0:T(8,128)} fusion(bf16[3072,9216]{1,0:T(8,128)(2,1)} %param.34, f32[9216]{0:T(1024)S(1)} %convert_element_type.192, bf16[1,384,3072]{2,1,0:T(8,128)(2,1)S(1)} %copy-done.8, f32[3072]{0:T(1024)S(1)} %bitcast.247, f32[384]{0:T(512)S(1)} %add_rsqrt_fusion.5, f32[384]{0:T(512)S(1)} %broadcast_multiply_fusion.4, ...), kind=kOutput, calls=%fused_computation.26 | convolution fusion | flops 21753888768 | bytes 73202688 | tf_op jit(solution)/shard_map/dot_general | solution.py:49
  79.1 13.0 %copy.63 = f32[48,8,72,128]{3,2,1,0:T(8,128)} copy(f32[48,8,72,128]{3,1,2,0:T(8,128)} %add_bitcast_fusion) | data formatting | bytes 28311552
  92.1 8.0 fusion.167
  100.0 4.1 slice.61
  104.1 6.3 copy.60
  113.4 36.1 %fusion.146 = f32[1,18432]{1,0:T(1,128)S(1)} fusion(bf16[3072,18432]{1,0:T(8,128)(2,1)} %param.44, bf16[1,3072]{1,0:T(2,128)(2,1)S(1)} %copy-done.12), kind=kOutput, calls=%fused_computation.186 | convolution fusion | flops 113264640 | bytes 113326080 | tf_op jit(solution)/shard_map/dot_general | solution.py:42
  151.1 27.1 %fusion.64 = f32[32,8,72,128]{3,1,2,0:T(8,128)} fusion(f32[9216]{0:T(1024)S(1)} %convert_element_type.188, bf16[3072,9216]{1,0:T(8,128)(2,1)} %param.46, bf16[1,256,3072]{2,1,0:T(8,128)(2,1)S(1)} %copy-done.6, f32[3072]{0:T(1024)S(1)} %bitcast.249, f32[256]{0:T(256)S(1)} %add_rsqrt_fusion.7, f32[256]{0:T(256)S(1)} %broadcast_multiply_fusion.6, ...), kind=kOutput, calls=%fused_computation.91 | convolution fusion | flops 14502592512 | bytes 67696640 | tf_op jit(solution)/shard_map/dot_general | solution.py:49
  178.3 5.4 copy.62
  184.1 3.2 copy-done.4
  195.2 3.6 copy-done
  201.5 63.0 %pmax.7 = f32[1,24,256]{2,0,1:T(1,128)S(1)} all-reduce(f32[1,24,256]{2,0,1:T(1,128)S(1)} %reduce_max.33), channel_id=1, replica_groups=mesh['dp'=2,'cp'=16] {'cp'}, use_global_device_ids=true, to_apply=%region_13.14 | all-reduce | flops 6144 | bytes 49152 | tf_op jit(solution)/shard_map/pmax | solution.py:87
  264.5 4.5 copy.57
  269.0 5.6 bitcast_multiply_fusion.1
  276.6 4.5 copy.44
  281.9 3.4 slice.60
  286.3 4.3 multiply_reduce_fusion.2
  290.6 2.9 copy.56
  294.8 6.2 copy.58
  314.1 64.2 %all-reduce.2.cloned.1.call-done = f32[1,256,24,129]{1,3,2,0:T(8,128)} async-done(((f32[1,256,24,129]{1,3,2,0:T(8,128)}), f32[1,256,24,129]{1,3,2,0:T(8,128)}) %all-reduce.2.cloned.1.call-update) | async-done | bytes 3170320 | tf_op jit(solution)/shard_map/psum | solution.py:90
  379.4 5.5 fusion.82
  384.9 9.2 fusion.172
  394.6 32.5 %fusion.27.clone.14 = bf16[256,12288]{1,0:T(8,128)(2,1)} fusion(bf16[3072,12288]{1,0:T(8,128)(2,1)} %param.52, f32[12288]{0:T(1024)S(1)} %convert_element_type.220, f32[1,256,3072]{2,1,0:T(8,128)S(1)} %get-tuple-element.42, f32[3072]{0:T(1024)S(1)} %bitcast.245, f32[256]{0:T(256)S(1)} %add_rsqrt_fusion.6, ...), kind=kOutput, calls=%fused_computation.34.clone.clone.clone.clone.clone.clone.clone.clone.clone.clone... | convolution fusion | flops 19362742272 | bytes 85010432 | tf_op jit(solution)/shard_map/dot_general | solution.py:62
  427.2 31.3 %fusion.61 = bf16[1,256,3072]{2,1,0:T(8,128)(2,1)} fusion(f32[1,256,3072]{2,1,0:T(8,128)S(1)} %get-tuple-element.42, bf16[12288,3072]{1,0:T(8,128)(2,1)} %param.54, f32[3072]{0:T(1024)S(1)} %copy-done.27, f32[3072]{0:T(1024)S(1)} %bitcast.244, bf16[256,12288]{1,0:T(8,128)(2,1)} %fusion.27.clone.14), kind=kOutput, calls=%fused_computation.88 | convolution fusion | flops 19330498560 | bytes 86532096 | tf_op jit(solution)/shard_map/dot_general | solution.py:64
  458.5 108.3 %all-gather.4.cloned.1.call-done = bf16[1,6144,24,128]{3,1,2,0:T(8,128)(2,1)} async-done(((bf16[1,384,24,128]{3,1,2,0:T(8,128)(2,1)}), bf16[1,6144,24,128]{3,1,2,0:T(8,128)(2,1)}) %all-gather.4.cloned.1.call-update) | async-done | bytes 37748752 | tf_op jit(solution)/shard_map/all_gather | solution.py:122
  566.7 93.9 %multiply_reduce_fusion = (f32[24,384]{1,0:T(8,128)S(1)}, f32[24,384,6400]{2,1,0:T(8,128)}) fusion(bf16[1,6144,24,128]{3,1,2,0:T(8,128)(2,1)} %all-gather.4.cloned.1.call-done, bf16[1,256,24,128]{3,1,2,0:T(8,128)(2,1)} %fusion.79, bf16[384,24,128]{0,1,2:T(8,128)(2,1)} %bitcast.227), kind=kOutput, calls=%fused_computation.1 | convolution fusion | flops 15296093184 | bytes 277647360 | tf_op jit(solution)/shard_map/bqhd,bkhd->bhqk/dot_general | solution.py:70
  660.6 71.0 %fusion = f32[24,384]{1,0:T(8,128)S(1)} fusion(f32[24,384,6400]{2,1,0:T(8,128)} %get-tuple-element.34, f32[24,384]{1,0:T(8,128)S(1)} %get-tuple-element.33), kind=kLoop, calls=%fused_computation.2 | loop fusion | flops 176937984 | bytes 236003328 | tf_op jit(solution)/shard_map/reduce_sum | solution.py:73
  731.7 24.1 %all-gather.6.cloned.1.call-done = bf16[1,6144,1,24,128]{1,4,3,2,0:T(8,128)(2,1)} async-done(((bf16[1,384,1,24,128]{1,4,3,2,0:T(8,128)(2,1)}), bf16[1,6144,1,24,128]{1,4,3,2,0:T(8,128)(2,1)}) %all-gather.6.cloned.1.call-update) | async-done | bytes 37748752 | tf_op jit(solution)/shard_map/all_gather | solution.py:123
  755.7 85.8 %fusion.51 = bf16[1,384,24,128]{1,3,2,0:T(8,128)(2,1)} fusion(f32[384,24]{0,1:T(8,128)S(1)} %bitcast.236, f32[24,384,6400]{2,1,0:T(8,128)} %get-tuple-element.34, f32[24,384]{1,0:T(8,128)S(1)} %get-tuple-element.33, bf16[1,6144,24,128]{1,3,2,0:T(8,128)(2,1)} %bitcast.251, bf16[1,256,24,128]{1,3,2,0:T(8,128)(2,1)} %bitcast.228), kind=kOutput, calls=%fused_computation.70 | convolution fusion | flops 15357444096 | bytes 277684224 | tf_op jit(solution)/shard_map/bhqk,bkhd->bqhd/dot_general | solution.py:74
  841.6 11.8 %fusion.171 = (f32[384]{0:T(512)S(1)}, f32[1,384,3072]{2,1,0:T(8,128)S(1)}) fusion(f32[3072]{0:T(1024)S(1)} %copy-done.26, bf16[384,3072]{0,1:T(8,128)(2,1)} %bitcast.252, bf16[3072,3072]{1,0:T(8,128)(2,1)} %param.38, f32[3072]{0:T(1024)S(1)} %bitcast.243, bf16[1,384,3072]{2,1,0:T(8,128)(2,1)S(1)} %copy-done.9), kind=kOutput, calls=%fused_computation.224 | convolution fusion | flops 7253655040 | bytes 28337664 | tf_op jit(solution)/shard_map/dot_general | solution.py:59
  856.3 43.7 %fusion.18.clone.6 = bf16[384,12288]{1,0:T(8,128)(2,1)} fusion(bf16[3072,12288]{1,0:T(8,128)(2,1)} %param.40, f32[12288]{0:T(1024)S(1)} %copy-done.13, f32[1,384,3072]{2,1,0:T(8,128)} %copy-done.10, f32[3072]{0:T(1024)S(1)} %bitcast.241, f32[384]{0:T(512)S(1)} %add_rsqrt_fusion.4, f32[384]{0:T(512)S(1)} %broadcast_multiply_fusion.3, ...), kind=kOutput, calls=%fused_computation.23.clone.clone.clone.clone.clone.1 | convolution fusion | flops 29044113408 | bytes 89730048 | tf_op jit(solution)/shard_map/dot_general | solution.py:62
  900.0 40.9 %fusion.52 = bf16[1,384,3072]{2,1,0:T(8,128)(2,1)} fusion(f32[1,384,3072]{2,1,0:T(8,128)} %copy-done.10, bf16[12288,3072]{1,0:T(8,128)(2,1)} %param.42, f32[3072]{0:T(1024)S(1)} %copy-done.25, f32[3072]{0:T(1024)S(1)} %bitcast.240, bf16[384,12288]{1,0:T(8,128)(2,1)} %fusion.18.clone.6), kind=kOutput, calls=%fused_computation.72 | convolution fusion | flops 28995747840 | bytes 92037120 | tf_op jit(solution)/shard_map/dot_general | solution.py:64
  (152 shorter events, 40.8 us)
Async XLA Ops:
  7.2 371.2 %all-reduce.2.cloned.1.call-start = ((), (), s32[]{:S(2)}) async-start(), calls=%async_computation.1 | async-start | bytes 6684672 | tf_op jit(solution)/shard_map/psum | solution.py:90
  8.3 37.3 %copy-start.14 = (bf16[18432]{0:T(1024)(128)(2,1)S(1)}, bf16[18432]{0:T(1024)(128)(2,1)}, u32[]{:S(2)}) copy-start(bf16[18432]{0:T(1024)(128)(2,1)} %param.33) | copy-start | bytes 110596
  8.3 37.9 %copy-start.8 = (bf16[1,384,3072]{2,1,0:T(8,128)(2,1)S(1)}, bf16[1,384,3072]{2,1,0:T(8,128)(2,1)}, u32[]{:S(2)}) copy-start(bf16[1,384,3072]{2,1,0:T(8,128)(2,1)} %param.28) | copy-start | bytes 7077892
  113.4 36.2 %copy-start.15 = (bf16[18432]{0:T(1024)(128)(2,1)S(1)}, bf16[18432]{0:T(1024)(128)(2,1)}, u32[]{:S(2)}) copy-start(bf16[18432]{0:T(1024)(128)(2,1)} %param.45) | copy-start | bytes 110596
  113.4 36.8 %copy-start.6 = (bf16[1,256,3072]{2,1,0:T(8,128)(2,1)S(1)}, bf16[1,256,3072]{2,1,0:T(8,128)(2,1)}, u32[]{:S(2)}) copy-start(bf16[1,256,3072]{2,1,0:T(8,128)(2,1)} %param.29) | copy-start | bytes 4718596
  113.4 37.7 %copy-start.17 = (bf16[9216]{0:T(1024)(128)(2,1)S(1)}, bf16[9216]{0:T(1024)(128)(2,1)}, u32[]{:S(2)}) copy-start(bf16[9216]{0:T(1024)(128)(2,1)} %param.47) | copy-start | bytes 55300
  183.6 3.6 copy-start.4
  183.6 4.5 copy-start.37
  183.7 4.5 copy-start.36
  187.3 5.4 copy-start.1
  195.2 3.7 copy-start
  276.6 290.2 %all-gather.4.cloned.1.call-start = ((), (), s32[]{:S(2)}) async-start(), calls=%async_computation | async-start | bytes 40108032 | tf_op jit(solution)/shard_map/all_gather | solution.py:122
  281.1 4.2 copy-start.38
  281.1 474.6 %all-gather.6.cloned.1.call-start = ((), (), s32[]{:S(2)}) async-start(), calls=%async_computation.2 | async-start | bytes 40108032 | tf_op jit(solution)/shard_map/all_gather | solution.py:123
  281.9 4.3 copy-start.2
  285.3 5.2 copy-start.32
  286.2 7.2 copy-start.29
  286.2 8.0 copy-start.30
  294.8 7.0 copy-start.31
  301.8 6.3 copy-start.3
  308.6 4.4 slice-start
  313.0 66.3 %copy-start.11 = (bf16[1,256,1,24,128]{1,4,3,2,0:T(8,128)(2,1)S(1)}, bf16[1,256,1,24,128]{1,4,3,2,0:T(8,128)(2,1)}, u32[]{:S(2)}) copy-start(bf16[1,256,1,24,128]{1,4,3,2,0:T(8,128)(2,1)} %copy.56) | copy-start | bytes 4718596
  379.4 5.5 copy-start.7
  384.8 9.7 %copy-start.23 = (f32[1,1,3072]{2,1,0:T(1,128)S(1)}, f32[1,1,3072]{2,1,0:T(1,128)}, u32[]{:S(2)}) copy-start(f32[1,1,3072]{2,1,0:T(1,128)} %get-tuple-element.20) | copy-start | bytes 36868
  384.8 9.7 %copy-start.24 = (f32[1,1,3072]{2,1,0:T(1,128)S(1)}, f32[1,1,3072]{2,1,0:T(1,128)}, u32[]{:S(2)}) copy-start(f32[1,1,3072]{2,1,0:T(1,128)} %get-tuple-element.21) | copy-start | bytes 36868
  394.6 32.6 %copy-start.22 = (f32[1,1,3072]{2,1,0:T(1,128)S(1)}, f32[1,1,3072]{2,1,0:T(1,128)}, u32[]{:S(2)}) copy-start(f32[1,1,3072]{2,1,0:T(1,128)} %get-tuple-element.19) | copy-start | bytes 36868
  394.6 32.6 %copy-start.27 = (f32[3072]{0:T(1024)S(1)}, f32[3072]{0:T(1024)}, u32[]{:S(2)}) copy-start(f32[3072]{0:T(1024)} %convert_element_type.222) | copy-start | bytes 36868
  755.7 85.8 %copy-start.9 = (bf16[1,384,3072]{2,1,0:T(8,128)(2,1)S(1)}, bf16[1,384,3072]{2,1,0:T(8,128)(2,1)}, u32[]{:S(2)}) copy-start(bf16[1,384,3072]{2,1,0:T(8,128)(2,1)} %param.28) | copy-start | bytes 7077892
  755.7 85.8 %copy-start.21 = (f32[1,1,3072]{2,1,0:T(1,128)S(1)}, f32[1,1,3072]{2,1,0:T(1,128)}, u32[]{:S(2)}) copy-start(f32[1,1,3072]{2,1,0:T(1,128)} %get-tuple-element.30) | copy-start | bytes 36868
  755.7 85.8 %copy-start.26 = (f32[3072]{0:T(1024)S(1)}, f32[3072]{0:T(1024)}, u32[]{:S(2)}) copy-start(f32[3072]{0:T(1024)} %convert_element_type.203) | copy-start | bytes 36868
  856.3 43.7 %copy-start.18 = (f32[1,1,3072]{2,1,0:T(1,128)S(1)}, f32[1,1,3072]{2,1,0:T(1,128)}, u32[]{:S(2)}) copy-start(f32[1,1,3072]{2,1,0:T(1,128)} %get-tuple-element.25) | copy-start | bytes 36868
  856.3 43.7 %copy-start.25 = (f32[3072]{0:T(1024)S(1)}, f32[3072]{0:T(1024)}, u32[]{:S(2)}) copy-start(f32[3072]{0:T(1024)} %convert_element_type.207) | copy-start | bytes 36868
  (12 other events, 32.8 us)
Sparse Core Ops, SparseCore 0:
  276.7 101.5 all-reduce.1
  379.9 186.8 all-gather.3
  568.3 187.3 all-gather.5
where the time goes:
time: 957 us; the launch traced here: 948 us
  matrix products  499 us (52%)
  waiting for transfers between devices  197 us (21%)
  other arithmetic  105 us (11%)
  local copies, waits for them, and re-layouts  68.6 us (7%)
  blocking collectives  63 us (7%)
  between operations  14.9 us (2%)
    all_gather x1, waiting for transfers between devices, device_fn(): img_k_all = lax.all_gather(img_k, 'cp', axis=1, tiled=True)  108 us
    dot_general x3, matrix products, partial_attend(): jnp.einsum('bqhd,bkhd->bhqk', queries, keys_all, preferred_element_type=j...  101 us
    dot_general x3, matrix products, partial_attend(): jnp.einsum('bhqk,bkhd->bqhd', exp_w.astype(jnp.bfloat16), vals_all, prefe...  96.8 us
    dot_general x2, matrix products, branch_out(): jnp.dot(normed, w_fc1, preferred_element_type=jnp.float32)  76.3 us
    reduce_sum x3, other arithmetic, partial_attend(): total = jnp.sum(exp_w, axis=-1)  74.7 us
    dot_general x2, matrix products, modulation(): jnp.dot(cond_act, w_mod, preferred_element_type=jnp.float32)  73.4 us
    dot_general x2, matrix products, branch_out(): jnp.dot(hidden, w_fc2, preferred_element_type=jnp.float32)  72.1 us
    psum x1, waiting for transfers between devices, text_attend(): packed = lax.psum(packed, 'cp')  64.2 us
  transfers between devices with their start and end apart: 3, of which 3 were waited for; matrix products, arithmetic and copies ran while one was open for 30% of the time, Pallas kernels for 0%

commit v1 on v0

v1 whole, which is shorter than its diff:
```python
import functools

import jax
import jax.numpy as jnp
from jax import lax
from jax.experimental import pallas as pl
from jax.experimental.pallas import tpu as pltpu
from jax.sharding import PartitionSpec as P

EPS = 1e-6
THETA = 10000.0
F32 = jnp.float32
BF16 = jnp.bfloat16
HD = 128
NCHIP = 8
NDEV = 16
VM = pl.BlockSpec(memory_space=pltpu.VMEM)
ANY = pl.BlockSpec(memory_space=pl.ANY)
MESH = pl.DeviceIdType.MESH
VMEM_LIMIT = 67043328


def dot(a, b):
    return jnp.dot(a, b, preferred_element_type=F32)


def dot_t(a, b):
    return lax.dot_general(a, b, (((1,), (1,)), ((), ())), preferred_element_type=F32)


def mod_kernel(cond_ref, wi_hbm, wt_hbm, out_ref, wi, wt, mine, lsem, ssem, rsem):
    me = lax.axis_index("cp")
    cols = wi.shape[1]
    n_row = cols // 128
    base = pl.multiple_of(me * cols, 128)
    ci = pltpu.make_async_copy(wi_hbm.at[:, pl.ds(base, cols)], wi, lsem.at[0])
    ct = pltpu.make_async_copy(wt_hbm.at[:, pl.ds(base, cols)], wt, lsem.at[1])
    ci.start()
    ct.start()
    barrier = pltpu.get_barrier_semaphore()
    for r in range(1, NDEV):
        peer = lax.rem(me + r, NDEV)
        pl.semaphore_signal(barrier, inc=1, device_id={"cp": peer}, device_id_type=MESH)
    c = cond_ref[...].astype(F32)
    act = (c * jax.nn.sigmoid(c)).astype(BF16)
    act = jnp.broadcast_to(act, (16, act.shape[1]))
    mine[...] = jnp.zeros_like(mine)
    ci.wait()
    ri = dot(act, wi[...])
    for i in range(n_row):
        mine[pl.ds(i, 1), :] = ri[0:1, i * 128:(i + 1) * 128]
    ct.wait()
    rt = dot(act, wt[...])
    for i in range(n_row):
        mine[pl.ds(n_row + i, 1), :] = rt[0:1, i * 128:(i + 1) * 128]
    out_ref[me] = mine[...]
    pl.semaphore_wait(barrier, NDEV - 1)
    copies = []
    for r in range(1, NDEV):
        peer = lax.rem(me + r, NDEV)
        cp = pltpu.make_async_remote_copy(
            src_ref=mine, dst_ref=out_ref.at[me], send_sem=ssem.at[r], recv_sem=rsem.at[r],
            device_id={"cp": peer}, device_id_type=MESH)
        cp.start()
        copies.append(cp)
    for cp in copies:
        cp.wait()


def modulation(cond_vec, w_img, w_txt):
    d, total = w_img.shape
    cols = total // NDEV
    n_row = cols // 128
    pad = -(-2 * n_row // 8) * 8
    out = pl.pallas_call(
        mod_kernel,
        out_shape=jax.ShapeDtypeStruct((NDEV, pad, 128), F32),
        in_specs=[VM, ANY, ANY],
        out_specs=VM,
        scratch_shapes=[
            pltpu.VMEM((d, cols), BF16), pltpu.VMEM((d, cols), BF16), pltpu.VMEM((pad, 128), F32),
            pltpu.SemaphoreType.DMA((2,)), pltpu.SemaphoreType.DMA((NDEV,)), pltpu.SemaphoreType.DMA((NDEV,)),
        ],
        compiler_params=pltpu.CompilerParams(collective_id=0, has_side_effects=True, vmem_limit_bytes=32 * 2**20),
        cost_estimate=pl.CostEstimate(flops=4 * d * cols * 16, bytes_accessed=4 * d * cols, transcendentals=0),
        name="mod",
    )(cond_vec, w_img, w_txt)
    img = out[:, :n_row].reshape(total)
    txt = out[:, n_row:2 * n_row].reshape(total)
    return img, txt


def ln_mod_rows(x, scale1p, shift):
    xf = x.astype(F32)
    mean = jnp.mean(xf, axis=-1, keepdims=True)
    cent = xf - mean
    var = jnp.mean(cent * cent, axis=-1, keepdims=True)
    return scale1p * (cent * lax.rsqrt(var + EPS)) + shift


def main_kernel(cfg, x_ref, xt_ref, mi_ref, mt_ref, wi_hbm, wt_hbm, bi_ref, bt_ref, gi_ref, gt_ref,
                cos_ref, se_ref, so_ref, o_hbm, ot_ref,
                u, w, ks, vs, qs, kb, vb, qb, s0, s1, mx0, mx1, ost, otmp,
                wsem, ssem, rsem, fssem, frsem, ossem, orsem):
    tok, txt, d_in, heads, ck = cfg
    hd_all = heads * HD
    nj = heads // NCHIP
    half = tok * NCHIP
    me = lax.axis_index("cp")
    chip, core = me // 2, me % 2
    sib = chip * 2 + (1 - core)

    def dev(c):
        return {"cp": c * 2 + core}

    barrier = pltpu.get_barrier_semaphore()
    for r in range(1, NCHIP):
        pl.semaphore_signal(barrier, inc=1, device_id=dev(lax.rem(chip + r, NCHIP)), device_id_type=MESH)
    pl.semaphore_signal(barrier, inc=1, device_id={"cp": sib}, device_id_type=MESH)

    wide = 4 * HD
    steps = []
    for j in range(nj):
        for kind in (1, 2, 0):
            for hf in range(2):
                steps.append(("img", kind, j, hf))
    for kind in (1, 2, 0):
        steps.append(("txt", kind, 0, 0))
    nslot = w.shape[0]

    def copies_of(n):
        where, kind, j, hf = steps[n]
        slot = n % nslot
        if where == "img":
            off = kind * hd_all + j * NCHIP * HD + hf * wide
            return [pltpu.make_async_copy(wi_hbm.at[:, pl.ds(off, wide)], w.at[slot], wsem.at[slot, 0])]
        out = []
        for jj in range(nj):
            off = pl.multiple_of(kind * hd_all + (jj * NCHIP + chip) * HD, HD)
            out.append(pltpu.make_async_copy(
                wt_hbm.at[:, pl.ds(off, HD)], w.at[slot, :, pl.ds(jj * HD, HD)], wsem.at[slot, jj]))
        return out

    for n in range(nslot - 1):
        for c in copies_of(n):
            c.start()

    rb = 16

    def ln_into(src, dst, m_ref, rows):
        shift = m_ref[0:1, :]
        scale = 1.0 + m_ref[1:2, :]

        def body(i, carry):
            sl = pl.ds(pl.multiple_of(i * rb, rb), rb)
            dst[sl, :] = ln_mod_rows(src[sl, :], scale, shift).astype(BF16)
            return carry
        lax.fori_loop(0, rows // rb, body, 0)

    ln_into(x_ref, u, mi_ref, tok)
    pl.semaphore_wait(barrier, NCHIP)

    def sends(kind, j):
        src, dst = ((qs, qb), (ks, kb), (vs, vb))[kind]
        out = []
        for r in range(1, NCHIP):
            c = lax.rem(chip + r, NCHIP)
            if kind == 0:
                d = dst.at[j, pl.ds(txt + chip * tok, tok)]
            elif kind == 1:
                d = dst.at[j, pl.ds(txt + core * half + chip * tok, tok)]
            else:
                d = dst.at[j, :, pl.ds(pl.multiple_of(txt + core * half + chip * tok, 128), tok)]
            out.append(pltpu.make_async_remote_copy(
                src_ref=src.at[j * NCHIP + c], dst_ref=d, send_sem=ssem.at[kind, j, r], recv_sem=rsem.at[kind, j, r],
                device_id=dev(c), device_id_type=MESH))
        return out

    def norm_rope(y, gain, cos, se, so, rope):
        ms = jnp.mean(y * y, axis=-1, keepdims=True)
        y = y * lax.rsqrt(ms + EPS) * gain
        if rope:
            y = y * cos + pltpu.roll(y, HD - 1, 1) * se + pltpu.roll(y, 1, 1) * so
        return y

    def img_step(n):
        _, kind, j, hf = steps[n]
        slot = n % nslot

        def body(i, carry):
            col = pl.multiple_of(i * 2 * HD, 2 * HD)
            boff = pl.multiple_of(kind * hd_all + j * NCHIP * HD + hf * wide + col, 2 * HD)
            y2 = dot(u[0:tok, :], w[slot, :, pl.ds(col, 2 * HD)])
            y2 = y2 + bi_ref[0:1, pl.ds(boff, 2 * HD)].astype(F32)
            for hh in range(2):
                head = j * NCHIP + hf * 4 + i * 2 + hh
                y = y2[:, hh * HD:(hh + 1) * HD]
                if kind == 2:
                    vs[head] = y.T.astype(BF16)
                else:
                    gain = gi_ref[kind:kind + 1, :].astype(F32)
                    y = norm_rope(y, gain, cos_ref[...], se_ref[...], so_ref[...], True)
                    (qs, ks)[kind][head] = y.astype(BF16)
            return carry
        lax.fori_loop(0, 2, body, 0)

    def txt_step(n):
        _, kind, _, _ = steps[n]
        slot = n % nslot
        y3 = dot(u[0:txt, :], w[slot, :, 0:nj * HD])
        for j in range(nj):
            boff = pl.multiple_of(kind * hd_all + (j * NCHIP + chip) * HD, HD)
            y = y3[:, j * HD:(j + 1) * HD] + bt_ref[0:1, pl.ds(boff, HD)].astype(F32)
            if kind == 2:
                vb[j, :, 0:txt] = y.T.astype(BF16)
            else:
                gain = gt_ref[kind:kind + 1, :].astype(F32)
                y = norm_rope(y, gain, None, None, None, False).astype(BF16)
                (qb, kb)[kind][j, 0:txt] = y

    def own_copy(kind, j):
        src = (qs, ks, vs)[kind]
        v = src[j * NCHIP + chip]
        if kind == 0:
            qb[j, pl.ds(txt + chip * tok, tok)] = v
        elif kind == 1:
            kb[j, pl.ds(txt + core * half + chip * tok, tok)] = v
        else:
            vb[j, :, pl.ds(pl.multiple_of(txt + core * half + chip * tok, 128), tok)] = v

    all_sends = []
    for n in range(len(steps)):
        nxt = n + nslot - 1
        if nxt < len(steps):
            for c in copies_of(nxt):
                c.start()
        for c in copies_of(n):
            c.wait()
        where, kind, j, hf = steps[n]
        if where == "img":
            img_step(n)
            if hf == 1:
                own_copy(kind, j)
                new = sends(kind, j)
                for c in new:
                    c.start()
                all_sends += new
        else:
            if kind == 1:
                ln_into(xt_ref, u, mt_ref, txt)
            txt_step(n)

    scale2 = (HD ** -0.5) * 1.4426950408889634
    keys = txt + 2 * half
    nchunk = keys // ck
    qt = 256
    ntile = (txt + half) // qt
    group = 2 * tok // qt
    ngroup = NCHIP // 2

    def tile_start(t):
        g = (t - 1) // group
        plane = lax.rem(chip // 2 + 1 + g, ngroup)
        row = txt + plane * (2 * tok) + lax.rem(t - 1, group) * qt
        return pl.multiple_of(jnp.where(t == 0, 0, row), 128)

    def qk(j, q, i, s_ref, mx):
        sl = pl.ds(pl.multiple_of(i * ck, ck), ck)
        s = dot_t(kb[j, sl], q)
        s_ref[sl, :] = s
        return jnp.maximum(mx, jnp.max(s.reshape(ck // 8, 8, qt), axis=0))

    def sm(j, i, s_ref, m, lsum, acc):
        sl = pl.ds(pl.multiple_of(i * ck, ck), ck)
        p = jnp.exp2((s_ref[sl, :] - m) * scale2)
        lsum = lsum + jnp.sum(p.reshape(ck // 8, 8, qt), axis=0)
        acc = acc + dot(vb[j, :, sl], p.astype(BF16))
        return lsum, acc

    def new_max():
        return jnp.full((8, qt), -jnp.inf, F32)

    def o_refs(j, c):
        src = ost.at[j, pl.ds(pl.multiple_of(c * tok, 128), tok)]
        dst = o_hbm.at[:, pl.ds(pl.multiple_of((j * NCHIP + chip) * HD, HD), HD)]
        return src, dst

    def o_remote(j, c):
        src, dst = o_refs(j, c)
        return pltpu.make_async_remote_copy(
            src_ref=src, dst_ref=dst, send_sem=ossem.at[j, c], recv_sem=orsem.at[j, chip],
            device_id=dev(c), device_id_type=MESH)

    def o_local(j):
        return pltpu.make_async_copy(*o_refs(j, chip), ossem.at[j, chip])

    def o_send(j, g):
        plane = lax.rem(chip // 2 + 1 + g, ngroup)
        for y in range(2):
            c = plane * 2 + y

            @pl.when(c != chip)
            def _():
                o_remote(j, c).start()

            @pl.when(c == chip)
            def _():
                o_local(j).start()

    def finish(j, t, lsum, acc):
        tot = jnp.sum(lsum, axis=0, keepdims=True)
        o = (acc / tot).T.astype(BF16)

        @pl.when(t == 0)
        def _():
            otmp[...] = o
            ot_ref[j] = otmp[pl.ds(pl.multiple_of(core * (txt // 2), 8), txt // 2), :]

        @pl.when(t > 0)
        def _():
            ost[j, pl.ds(pl.multiple_of(tile_start(t) - txt, 128), qt)] = o

            @pl.when(lax.rem(t, group) == 0)
            def _():
                o_send(j, t // group - 1)

    def pair(j, t, s_cur, mx_cur, s_nxt, mx_nxt, has_next):
        m = jnp.max(mx_cur[...], axis=0, keepdims=True)
        lsum = jnp.zeros((8, qt), F32)
        acc = jnp.zeros((HD, qt), F32)
        if has_next:
            q = qb[j, pl.ds(tile_start(t + 1), qt)]

            def body(i, carry):
                lsum, acc, mx = carry
                mx = qk(j, q, i, s_nxt, mx)
                lsum, acc = sm(j, i, s_cur, m, lsum, acc)
                return lsum, acc, mx
            lsum, acc, mx = lax.fori_loop(0, nchunk, body, (lsum, acc, new_max()))
            mx_nxt[...] = mx
        else:
            def body(i, carry):
                return sm(j, i, s_cur, m, *carry)
            lsum, acc = lax.fori_loop(0, nchunk, body, (lsum, acc))
        finish(j, t, lsum, acc)

    for j in range(nj):
        recv = {kind: sends(kind, j) for kind in (0, 1, 2)}
        fwd = []
        for kind in (1, 2):
            for c in recv[kind]:
                c.wait_recv()
            if kind == 1:
                ref = kb.at[j, pl.ds(txt + core * half, half)]
            else:
                ref = vb.at[j, :, pl.ds(pl.multiple_of(txt + core * half, 128), half)]
            f = pltpu.make_async_remote_copy(
                src_ref=ref, dst_ref=ref, send_sem=fssem.at[kind - 1, j], recv_sem=frsem.at[kind - 1, j],
                device_id={"cp": sib}, device_id_type=MESH)
            f.start()
            fwd.append(f)
        for c in recv[0]:
            c.wait_recv()
        for f in fwd:
            f.wait()

        q = qb[j, 0:qt]

        def first(i, mx):
            return qk(j, q, i, s0, mx)
        mx0[...] = lax.fori_loop(0, nchunk, first, new_max())

        def two(i, carry):
            pair(j, 2 * i, s0, mx0, s1, mx1, True)
            pair(j, 2 * i + 1, s1, mx1, s0, mx0, True)
            return carry
        lax.fori_loop(0, (ntile - 1) // 2, two, 0)
        pair(j, jnp.int32(ntile - 1), s0, mx0, s1, mx1, False)

    for c in all_sends:
        c.wait_send()
    for j in range(nj):
        o_local(j).wait()
        for r in range(1, NCHIP):
            c = lax.rem(chip + r, NCHIP)
            o_remote(j, c).wait_send()
            src, _ = o_refs(j, c)
            arrived = o_hbm.at[:, pl.ds(pl.multiple_of((j * NCHIP + c) * HD, HD), HD)]
            pltpu.make_async_remote_copy(
                src_ref=src, dst_ref=arrived, send_sem=ossem.at[j, c], recv_sem=orsem.at[j, c],
                device_id=dev(c), device_id_type=MESH).wait_recv()


def attention(image, text, m_img, m_txt, w_img, w_txt, b_img, b_txt, g_img, g_txt, cos, se, so):
    tok, d_in = image.shape
    txt = text.shape[0]
    hd_all = w_img.shape[1] // 3
    heads = hd_all // HD
    nj = heads // NCHIP
    half = tok * NCHIP
    keys = txt + 2 * half
    ck = 1280 if keys % 1280 == 0 else 256
    nslot = 3
    cfg = (tok, txt, d_in, heads, ck)
    dma = pltpu.SemaphoreType.DMA
    flops = 2 * tok * d_in * 3 * hd_all + 4 * nj * HD * (half + txt) * keys
    return pl.pallas_call(
        functools.partial(main_kernel, cfg),
        out_shape=(jax.ShapeDtypeStruct((tok, hd_all), BF16), jax.ShapeDtypeStruct((nj, txt // 2, HD), BF16)),
        in_specs=[VM, VM, VM, VM, ANY, ANY] + [VM] * 7,
        out_specs=(ANY, VM),
        scratch_shapes=[
            pltpu.VMEM((max(tok, txt), d_in), BF16),
            pltpu.VMEM((nslot, d_in, 4 * HD), BF16),
            pltpu.VMEM((heads, tok, HD), BF16),
            pltpu.VMEM((heads, HD, tok), BF16),
            pltpu.VMEM((heads, tok, HD), BF16),
            pltpu.VMEM((nj, keys, HD), BF16),
            pltpu.VMEM((nj, HD, keys), BF16),
            pltpu.VMEM((nj, txt + half, HD), BF16),
            pltpu.VMEM((keys, 256), F32),
            pltpu.VMEM((keys, 256), F32),
            pltpu.VMEM((8, 256), F32),
            pltpu.VMEM((8, 256), F32),
            pltpu.VMEM((nj, half, HD), BF16),
            pltpu.VMEM((txt, HD), BF16),
            dma((nslot, nj)), dma((3, nj, NCHIP)), dma((3, nj, NCHIP)), dma((2, nj)), dma((2, nj)),
            dma((nj, NCHIP)), dma((nj, NCHIP)),
        ],
        compiler_params=pltpu.CompilerParams(collective_id=1, has_side_effects=True, vmem_limit_bytes=VMEM_LIMIT),
        cost_estimate=pl.CostEstimate(flops=flops, bytes_accessed=2 * d_in * 3 * hd_all, transcendentals=0),
        name="attn",
    )(image, text, m_img, m_txt, w_img, w_txt, b_img, b_txt, g_img, g_txt, cos, se, so)


def proj_kernel(o_ref, x_ref, m_ref, w_ref, b_ref, h_ref, z_ref):
    i = pl.program_id(0)
    nb = w_ref.shape[1]
    col = pl.multiple_of(i * nb, nb)
    sl = pl.ds(col, nb)
    y = dot(o_ref[...], w_ref[...]) + b_ref[0:1, sl].astype(F32)
    h_ref[:, sl] = x_ref[:, sl].astype(F32) + m_ref[2:3, sl] * y

    @pl.when(i == pl.num_programs(0) - 1)
    def _():
        shift, scale = m_ref[3:4, :], 1.0 + m_ref[4:5, :]
        rb = 16

        def body(k, carry):
            rows = pl.ds(pl.multiple_of(k * rb, rb), rb)
            z_ref[rows, :] = ln_mod_rows(h_ref[rows, :], scale, shift).astype(BF16)
            return carry
        lax.fori_loop(0, h_ref.shape[0] // rb, body, 0)


def out_proj(o, x, mods, w, b):
    tok, d = x.shape
    nb = 512
    full = lambda i: (0, 0)
    return pl.pallas_call(
        proj_kernel,
        grid=(d // nb,),
        out_shape=(jax.ShapeDtypeStruct((tok, d), F32), jax.ShapeDtypeStruct((tok, d), BF16)),
        in_specs=[pl.BlockSpec((tok, o.shape[1]), full), pl.BlockSpec((tok, d), full), pl.BlockSpec(mods.shape, full),
                  pl.BlockSpec((w.shape[0], nb), lambda i: (0, i)), pl.BlockSpec(b.shape, full)],
        out_specs=(pl.BlockSpec((tok, d), full), pl.BlockSpec((tok, d), full)),
        compiler_params=pltpu.CompilerParams(dimension_semantics=("arbitrary",), vmem_limit_bytes=48 * 2**20),
        cost_estimate=pl.CostEstimate(flops=2 * tok * d * d, bytes_accessed=2 * d * d, transcendentals=0),
        name="img_proj",
    )(o, x, mods, w, b)


def gelu(x):
    return 0.5 * x * (1.0 + jnp.tanh(0.7978845608028654 * (x + 0.044715 * (x * x * x))))


def ffn_kernel(last, z_ref, h_ref, m_ref, w1_ref, b1_ref, w2_ref, b2_ref, *rest):
    i = pl.program_id(0)
    n = pl.num_programs(0)
    if last:
        acc_in, out_ref, acc = rest
    else:
        (acc,) = rest
        acc_in = None
    a = dot(z_ref[...], w1_ref[...]) + b1_ref[...].astype(F32)
    a = gelu(a).astype(BF16)

    @pl.when(i == 0)
    def _():
        base = b2_ref[...].astype(F32) if acc_in is None else acc_in[...]
        acc[...] = base + dot(a, w2_ref[...])

    @pl.when(i > 0)
    def _():
        acc[...] += dot(a, w2_ref[...])

    if last:
        @pl.when(i == n - 1)
        def _():
            out_ref[...] = (h_ref[...] + m_ref[5:6, :] * acc[...]).astype(BF16)


def ffn(z, h, mods, w1, b1, w2, b2, lo, hi, acc_in=None):
    tok, d = z.shape
    ff = w1.shape[1]
    nb = 512
    lo, hi = lo // nb, hi // nb
    full = lambda i: (0, 0)
    last = acc_in is not None
    specs = [pl.BlockSpec((tok, d), full), pl.BlockSpec((tok, d), full), pl.BlockSpec(mods.shape, full),
             pl.BlockSpec((d, nb), lambda i: (0, i + lo)), pl.BlockSpec((1, nb), lambda i: (0, i + lo)),
             pl.BlockSpec((nb, d), lambda i: (i + lo, 0)), pl.BlockSpec((1, d), full)]
    args = [z, h, mods, w1, b1, w2, b2]
    if last:
        specs.append(pl.BlockSpec((tok, d), full))
        args.append(acc_in)
    return pl.pallas_call(
        functools.partial(ffn_kernel, last),
        grid=(hi - lo,),
        out_shape=jax.ShapeDtypeStruct((tok, d), BF16 if last else F32),
        in_specs=specs,
        out_specs=pl.BlockSpec((tok, d), full),
        scratch_shapes=[pltpu.VMEM((tok, d), F32)] if last else [],
        compiler_params=pltpu.CompilerParams(dimension_semantics=("arbitrary",), vmem_limit_bytes=VMEM_LIMIT),
        cost_estimate=pl.CostEstimate(flops=4 * tok * d * (hi - lo) * nb, bytes_accessed=4 * d * (hi - lo) * nb,
                                      transcendentals=tok * (hi - lo) * nb),
        name="img_ffn",
    )(*args)


def txt_kernel(og_ref, x_ref, m_ref, wp_hbm, bp_ref, w1_hbm, b1_ref, w2_hbm, h_ref, part_ref,
               o, h, wp, w1, w2, z, a, sem, psem):
    me = lax.axis_index("cp")
    txt, d = x_ref.shape
    fb = w1.shape[1]
    nj = og_ref.shape[1]
    nb = wp.shape[2]
    c1 = pltpu.make_async_copy(w1_hbm.at[:, pl.ds(pl.multiple_of(me * fb, 128), fb)], w1, sem.at[0])
    c2 = pltpu.make_async_copy(w2_hbm.at[pl.ds(pl.multiple_of(me * fb, 128), fb), :], w2, sem.at[1])

    def cp(i, slot):
        return pltpu.make_async_copy(wp_hbm.at[:, pl.ds(pl.multiple_of(i * nb, nb), nb)], wp.at[slot], psem.at[slot])

    nstep = d // nb
    cp(0, 0).start()
    c1.start()
    c2.start()
    rows = txt // 2
    for c in range(NCHIP):
        for k in range(2):
            for j in range(nj):
                o[k * rows:(k + 1) * rows, (j * NCHIP + c) * HD:(j * NCHIP + c + 1) * HD] = og_ref[c * 2 + k, j]

    def body(i, carry):
        slot = lax.rem(i, 2)

        @pl.when(i + 1 < nstep)
        def _():
            cp(i + 1, 1 - slot).start()
        cp(i, slot).wait()
        sl = pl.ds(pl.multiple_of(i * nb, nb), nb)
        y = dot(o[...], wp[slot]) + bp_ref[0:1, sl].astype(F32)
        h[:, sl] = x_ref[:, sl].astype(F32) + m_ref[2:3, sl] * y
        return carry
    lax.fori_loop(0, nstep, body, 0)
    shift, scale = m_ref[3:4, :], 1.0 + m_ref[4:5, :]
    rb = 16

    def lnb(k, carry):
        r = pl.ds(pl.multiple_of(k * rb, rb), rb)
        z[r, :] = ln_mod_rows(h[r, :], scale, shift).astype(BF16)
        return carry
    lax.fori_loop(0, txt // rb, lnb, 0)
    h_ref[...] = h[pl.ds(pl.multiple_of(me * (txt // NDEV), 8), txt // NDEV), :]
    c1.wait()
    y = dot(z[...], w1[...]) + b1_ref[0:1, pl.ds(pl.multiple_of(me * fb, 128), fb)].astype(F32)
    a[...] = gelu(y).astype(BF16)
    c2.wait()

    def fc2(i, carry):
        sl = pl.ds(pl.multiple_of(i * nb, nb), nb)
        part_ref[:, sl] = dot(a[...], w2[:, sl])
        return carry
    lax.fori_loop(0, nstep, fc2, 0)


def text_mlp(og, x, mods, wp, bp, w1, b1, w2):
    txt, d = x.shape
    ff = w1.shape[1]
    fb = ff // NDEV
    nb = 512
    dma = pltpu.SemaphoreType.DMA
    return pl.pallas_call(
        txt_kernel,
        out_shape=(jax.ShapeDtypeStruct((txt // NDEV, d), F32), jax.ShapeDtypeStruct((txt, d), F32)),
        in_specs=[VM, VM, VM, ANY, VM, ANY, VM, ANY],
        out_specs=(VM, VM),
        scratch_shapes=[
            pltpu.VMEM((txt, wp.shape[0]), BF16), pltpu.VMEM((txt, d), F32), pltpu.VMEM((2, wp.shape[0], nb), BF16),
            pltpu.VMEM((d, fb), BF16), pltpu.VMEM((fb, d), BF16), pltpu.VMEM((txt, d), BF16), pltpu.VMEM((txt, fb), BF16),
            dma((2,)), dma((2,)),
        ],
        compiler_params=pltpu.CompilerParams(vmem_limit_bytes=48 * 2**20),
        cost_estimate=pl.CostEstimate(flops=2 * txt * d * (d + 2 * fb), bytes_accessed=2 * d * (d + 2 * fb), transcendentals=0),
        name="txt_mlp",
    )(og, x, mods, wp, bp, w1, b1, w2)


def rope_tables(ids):
    d_t = HD // 8
    d_s = (HD - d_t) // 2
    pos = ids.astype(F32)
    lanes = []
    for axis, width in enumerate((d_t, d_s, d_s)):
        omega = THETA ** (-jnp.arange(0, width, 2, dtype=F32) / width)
        lanes.append(pos[:, axis:axis + 1] * jnp.repeat(omega, 2)[None, :])
    ang = jnp.concatenate(lanes, axis=-1)
    odd = (jnp.arange(HD) % 2).astype(F32)[None, :]
    sin = jnp.sin(ang)
    return jnp.cos(ang), -sin * (1.0 - odd), sin * odd


def device_fn(image, text, cond_vec, image_ids, *weights):
    (wm, bm, wqkv, bqkv, qg, kg, wp, bp, w1, b1, w2, b2) = weights[:12]
    (twm, tbm, twqkv, tbqkv, tqg, tkg, twp, tbp, tw1, tb1, tw2, tb2) = weights[12:]
    x, xt = image[0], text[0]
    d = x.shape[1]
    row = lambda v: v[None, :]
    m_img, m_txt = modulation(cond_vec, wm, twm)
    m_img = (m_img + bm.astype(F32)).reshape(6, d)
    m_txt = (m_txt + tbm.astype(F32)).reshape(6, d)
    cos, se, so = rope_tables(image_ids)
    o_img, o_txt = attention(x, xt, m_img, m_txt, wqkv, twqkv, row(bqkv), row(tbqkv),
                             jnp.stack([qg, kg]), jnp.stack([tqg, tkg]), cos, se, so)
    og = lax.all_gather(o_txt, "cp")
    h, z = out_proj(o_img, x, m_img, wp, row(bp))
    ht, part = text_mlp(og, xt, m_txt, twp, row(tbp), tw1, row(tb1), tw2)
    ff = w1.shape[1]
    acc = ffn(z, h, m_img, w1, row(b1), w2, row(b2), 0, ff // 2)
    red = lax.psum_scatter(part, "cp", scatter_dimension=0, tiled=True)
    rows = (ht + m_txt[5:6] * (red + tb2.astype(F32)[None, :])).astype(BF16)
    text_out = lax.all_gather(rows, "cp", tiled=True)
    image_out = ffn(z, h, m_img, w1, row(b1), w2, row(b2), ff // 2, ff, acc)
    return image_out[None], text_out[None]


def solution(mesh):
    act = P("dp", "cp", None)
    txt = P("dp", None, None)
    in_specs = (act, txt, P("dp", None), P(("dp", "cp"), None)) + (P(),) * 24
    return jax.shard_map(device_fn, mesh=mesh, in_specs=in_specs, out_specs=(act, txt), check_vma=False)
```

time: 957 us -> 492 us (0.51)
  matrix products: 499 us -> 0 us
  Pallas kernels: 0 us -> 368 us
  waiting for transfers between devices: 197 us -> 87.6 us
  other arithmetic: 105 us -> 4.18 us
  blocking collectives: 63 us -> 0 us
  local copies, waits for them, and re-layouts: 68.6 us -> 14.3 us
    dot_general x16 -> x0, matrix products: 499 us -> none  [the longest x3 101 us: partial_attend(): jnp.einsum('bqhd,bkhd->bhqk', queries, keys_all, preferred_element_type=j...]
    pallas_call x0 -> x6, Pallas kernels: none -> 368 us  [the longest x1 223 us: attention(): pl.pallas_call(functools.partial(main_kernel, cfg), out_shape=(jax.ShapeD...]
    all_gather x2, waiting for transfers between devices: 132 us -> 45.4 us  [the longest x1 45.4 us: device_fn(): og = lax.all_gather(o_txt, 'cp')]
    reduce_sum x13 -> x0, other arithmetic: 85 us -> none  [the longest x3 74.7 us: partial_attend(): total = jnp.sum(exp_w, axis=-1)]
    psum x1 -> x0, waiting for transfers between devices: 64.2 us -> none  [text_attend(): packed = lax.psum(packed, 'cp')]
    pmax x1 -> x0, blocking collectives: 63 us -> none  [text_attend(): peak_all = lax.pmax(img_peak, 'cp')]
    reduce_scatter x0 -> x1, waiting for transfers between devices: none -> 42.1 us  [device_fn(): red = lax.psum_scatter(part, 'cp', scatter_dimension=0, tiled=True)]
    unnamed x92 -> x43, local copies, waits for them, and re-layouts: 47.3 us -> 8.53 us
  transfers between devices with their start and end apart: 3 -> 3, of which waited for: 3 -> 2; matrix products, arithmetic and copies ran while one was open for 30% -> 1% of each run, Pallas kernels for 0% -> 22%
where the time goes in v1:
time: 492 us; the launch traced here: 489 us
  Pallas kernels  368 us (75%)
  waiting for transfers between devices  87.6 us (18%)
  between operations  14.5 us (3%)
  local copies, waits for them, and re-layouts  14.3 us (3%)
    pallas_call x1, Pallas kernels, attention(): pl.pallas_call(functools.partial(main_kernel, cfg), out_shape=(jax.ShapeD...  223 us
    pallas_call x2, Pallas kernels, ffn(): pl.pallas_call(functools.partial(ffn_kernel, last), grid=(hi - lo,), out_...  87.1 us
    all_gather x1, waiting for transfers between devices, device_fn(): og = lax.all_gather(o_txt, 'cp')  45.4 us
    reduce_scatter x1, waiting for transfers between devices, device_fn(): red = lax.psum_scatter(part, 'cp', scatter_dimension=0, tiled=True)  42.1 us
    pallas_call x1, Pallas kernels, text_mlp(): pl.pallas_call(txt_kernel, out_shape=(jax.ShapeDtypeStruct((txt // NDEV,...  22.7 us
    pallas_call x1, Pallas kernels, out_proj(): pl.pallas_call(proj_kernel, grid=(d // nb,), out_shape=(jax.ShapeDtypeStr...  20.5 us
    pallas_call x1, Pallas kernels, modulation(): pl.pallas_call(mod_kernel, out_shape=jax.ShapeDtypeStruct((NDEV, pad, 128...  14.5 us
  transfers between devices with their start and end apart: 3, of which 2 were waited for; matrix products, arithmetic and copies ran while one was open for 1% of the time, Pallas kernels for 22%

profile of v1, /device:TPU:0, one launch (start us, length us, event | category | flops | bytes accessed | tf_op | source)
XLA Modules:
  0.0 488.8 jit_solution(5816932474745699113)
XLA Ops:
  7.3 0.7 copy-done.5
  8.0 14.5 %mod.1 = f32[16,24,128]{2,1,0:T(8,128)S(1)} custom-call(bf16[1,3072]{1,0:T(2,128)(2,1)S(1)} %copy-done.5, bf16[3072,18432]{1,0:T(8,128)(2,1)} %wi_hbm.2, bf16[3072,18432]{1,0:T(8,128)(2,1)} %wt_hbm.2), custom_call_target="tpu_custom_call" | custom-call | flops 226492416 | bytes 14155776 | tf_op jit(solution)/shard_map/mod/pallas_call | solution.py:75
  22.7 0.7 reshape.36.mi_ref.m_ref
  23.4 0.7 reshape.38.mt_ref.m_ref
  24.0 0.6 broadcast_in_dim.40.bi_ref
  24.7 0.6 broadcast_in_dim.41.bt_ref
  25.3 0.1 broadcast_in_dim.43
  25.4 0.1 mul.93
  25.5 0.1 broadcast_in_dim.42
  25.6 0.1 mul.87
  25.7 0.1 broadcast_multiply_fusion.3
  25.8 0.2 broadcast_multiply_fusion.2
  26.0 0.6 pad_maximum_fusion.1
  26.6 1.6 broadcast_multiply_fusion
  28.3 223.1 %attn.1 = (bf16[384,3072]{1,0:T(8,128)(2,1)}, bf16[3,128,128]{2,1,0:T(8,128)(2,1)}) custom-call(bf16[384,3072]{1,0:T(8,128)(2,1)} %bitcast.18, bf16[256,3072]{1,0:T(8,128)(2,1)} %bitcast.9, f32[6,3072]{1,0:T(8,128)} %reshape.36.mi_ref.m_ref, f32[6,3072]{1,0:T(8,128)} %reshape.38.mt_ref.m_ref, bf16[3072,9216]{1,0:T(8,128)(2,1)} %wi_hbm.3, ...), custom_call_target="tpu_custom_call" | custom-call | flops 54458843136 | bytes 56623104 | tf_op jit(solution)/shard_map/attn/pallas_call | solution.py:407
  251.4 0.3 reduce-scatter.2.cloned.1.call-start
  251.7 0.7 broadcast_in_dim.48.bp_ref
  252.4 0.8 broadcast_in_dim.49.b1_ref
  253.2 45.4 %all-gather.6.cloned.1.call-done = bf16[48,128,128]{2,1,0:T(8,128)(2,1)} async-done(((bf16[3,128,128]{2,1,0:T(8,128)(2,1)}), bf16[48,128,128]{2,1,0:T(8,128)(2,1)}) %all-gather.6.cloned.1.call-update) | async-done | bytes 1572880 | tf_op jit(solution)/shard_map/all_gather | solution.py:635
  298.6 1.4 copy-done.1
  300.0 1.4 copy-done.2
  301.4 0.9 copy-done.4
  302.3 22.7 %txt_mlp.1 = (f32[16,3072]{1,0:T(8,128)S(1)}, f32[256,3072]{1,0:T(8,128)}) custom-call(bf16[16,3,128,128]{3,2,1,0:T(8,128)(2,1)S(1)} %bitcast.11, bf16[256,3072]{1,0:T(8,128)(2,1)S(1)} %bitcast.10, f32[6,3072]{1,0:T(8,128)S(1)} %copy-done.4, bf16[3072,3072]{1,0:T(8,128)(2,1)} %wp_hbm.1, bf16[1,3072]{1,0:T(2,128)(2,1)S(1)} %broadcast_in_dim.48.bp_ref, ...), custom_call_target="tpu_custom_call" | custom-call | flops 7247757312 | bytes 28311552 | tf_op jit(solution)/shard_map/txt_mlp/pallas_call | solution.py:593
  325.2 0.6 broadcast_in_dim.45.b1_ref
  325.8 0.6 broadcast_in_dim.46.b2_ref
  326.4 20.5 %img_proj.1 = (f32[384,3072]{1,0:T(8,128)}, bf16[384,3072]{1,0:T(8,128)(2,1)S(1)}) custom-call(bf16[384,3072]{1,0:T(8,128)(2,1)S(1)} %copy-done.6, bf16[384,3072]{1,0:T(8,128)(2,1)} %bitcast.19, f32[6,3072]{1,0:T(8,128)S(1)} %copy-done.3, bf16[3072,3072]{1,0:T(8,128)(2,1)} %w_ref.1, bf16[1,3072]{1,0:T(2,128)(2,1)S(1)} %broadcast_in_dim.44.b_ref), custom_call_target="tpu_custom_call" | custom-call | flops 7247757312 | bytes 18874368 | tf_op jit(solution)/shard_map/img_proj/pallas_call | solution.py:460
  346.9 1.4 copy-done
  348.3 42.1 %reduce-scatter.2.cloned.1.call-done = f32[16,3072]{1,0:T(8,128)} async-done(((f32[256,3072]{1,0:T(8,128)}), f32[16,3072]{1,0:T(8,128)}) %reduce-scatter.2.cloned.1.call-update) | async-done | bytes 196624 | tf_op jit(solution)/shard_map/reduce_scatter | solution.py:640
  390.4 1.6 add_convert_fusion
  392.1 43.0 %img_ffn.2.rest_0_ = f32[384,3072]{1,0:T(8,128)} custom-call(bf16[384,3072]{1,0:T(8,128)(2,1)} %copy-done, f32[384,3072]{1,0:T(8,128)} %get-tuple-element.10.h_ref, f32[6,3072]{1,0:T(8,128)} %reshape.36.mi_ref.m_ref, bf16[3072,12288]{1,0:T(8,128)(2,1)} %w1_ref.3, bf16[1,12288]{1,0:T(2,128)(2,1)} %broadcast_in_dim.45.b1_ref, bf16[12288,3072]{1,0:T(8,128)(2,1)} %w2_ref.3, ...), custom_call_target="tpu_custom_call" | custom-call | flops 28991029248 | bytes 75497472 | tf_op jit(solution)/shard_map/img_ffn/pallas_call | solution.py:517
  435.0 44.1 %img_ffn.3 = bf16[384,3072]{1,0:T(8,128)(2,1)} custom-call(bf16[384,3072]{1,0:T(8,128)(2,1)} %copy-done, f32[384,3072]{1,0:T(8,128)} %get-tuple-element.10.h_ref, f32[6,3072]{1,0:T(8,128)} %reshape.36.mi_ref.m_ref, bf16[3072,12288]{1,0:T(8,128)(2,1)} %w1_ref.3, bf16[1,12288]{1,0:T(2,128)(2,1)} %broadcast_in_dim.45.b1_ref, bf16[12288,3072]{1,0:T(8,128)(2,1)} %w2_ref.3, ...), custom_call_target="tpu_custom_call" | custom-call | flops 28991029248 | bytes 75497472 | tf_op jit(solution)/shard_map/img_ffn/pallas_call | solution.py:517
  479.1 2.7 copy.31
  (58 shorter events, 0.4 us)
Async XLA Ops:
  7.2 291.4 %all-gather.6.cloned.1.call-start = ((), (), s32[]{:S(2)}) async-start(), calls=%async_computation.3 | async-start | bytes 1671168 | tf_op jit(solution)/shard_map/all_gather | solution.py:635
  7.3 0.7 copy-start.5
  8.0 14.7 %copy-start.8 = (bf16[18432]{0:T(1024)(128)(2,1)S(1)}, bf16[18432]{0:T(1024)(128)(2,1)}, u32[]{:S(2)}) copy-start(bf16[18432]{0:T(1024)(128)(2,1)} %param.33) | copy-start | bytes 110596
  8.0 15.4 %copy-start.9 = (bf16[18432]{0:T(1024)(128)(2,1)S(1)}, bf16[18432]{0:T(1024)(128)(2,1)}, u32[]{:S(2)}) copy-start(bf16[18432]{0:T(1024)(128)(2,1)} %param.45) | copy-start | bytes 110596
  8.0 16.1 %copy-start.11 = (bf16[9216]{0:T(1024)(128)(2,1)S(1)}, bf16[9216]{0:T(1024)(128)(2,1)}, u32[]{:S(2)}) copy-start(bf16[9216]{0:T(1024)(128)(2,1)} %param.35) | copy-start | bytes 55300
  8.0 16.7 %copy-start.12 = (bf16[9216]{0:T(1024)(128)(2,1)S(1)}, bf16[9216]{0:T(1024)(128)(2,1)}, u32[]{:S(2)}) copy-start(bf16[9216]{0:T(1024)(128)(2,1)} %param.47) | copy-start | bytes 55300
  8.0 17.5 %copy-start.13 = (s32[384,3]{0,1:T(4,128)S(1)}, s32[384,3]{0,1:T(4,128)}, u32[]{:S(2)}) copy-start(s32[384,3]{0,1:T(4,128)} %param.31) | copy-start | bytes 13828
  8.0 18.0 %copy-start.17 = (bf16[128]{0:T(256)(128)(2,1)S(1)}, bf16[128]{0:T(256)(128)(2,1)}, u32[]{:S(2)}) copy-start(bf16[128]{0:T(256)(128)(2,1)} %param.37) | copy-start | bytes 772
  8.0 18.0 %copy-start.18 = (bf16[128]{0:T(256)(128)(2,1)S(1)}, bf16[128]{0:T(256)(128)(2,1)}, u32[]{:S(2)}) copy-start(bf16[128]{0:T(256)(128)(2,1)} %param.36) | copy-start | bytes 772
  8.0 18.0 %copy-start.19 = (bf16[128]{0:T(256)(128)(2,1)S(1)}, bf16[128]{0:T(256)(128)(2,1)}, u32[]{:S(2)}) copy-start(bf16[128]{0:T(256)(128)(2,1)} %param.49) | copy-start | bytes 772
  8.0 18.0 %copy-start.20 = (bf16[128]{0:T(256)(128)(2,1)S(1)}, bf16[128]{0:T(256)(128)(2,1)}, u32[]{:S(2)}) copy-start(bf16[128]{0:T(256)(128)(2,1)} %param.48) | copy-start | bytes 772
  23.4 4.9 %copy-start.7 = (f32[18432]{0:T(1024)}, f32[18432]{0:T(1024)S(1)}, u32[]{:S(2)}) copy-start(f32[18432]{0:T(1024)S(1)} %convert_add_fusion) | copy-start | bytes 221188
  251.4 139.0 %reduce-scatter.2.cloned.1.call-start = ((), (), s32[]{:S(2)}) async-start(), calls=%async_computation.1 | async-start | bytes 3342336 | tf_op jit(solution)/shard_map/reduce_scatter | solution.py:640
  298.6 1.4 copy-start.1
  300.0 1.4 copy-start.2
  301.4 0.9 copy-start.4
  302.3 22.8 %copy-start.14 = (bf16[3072]{0:T(1024)(128)(2,1)S(1)}, bf16[3072]{0:T(1024)(128)(2,1)}, u32[]{:S(2)}) copy-start(bf16[3072]{0:T(1024)(128)(2,1)} %param.39) | copy-start | bytes 18436
  302.3 22.9 %copy-start.10 = (bf16[12288]{0:T(1024)(128)(2,1)S(1)}, bf16[12288]{0:T(1024)(128)(2,1)}, u32[]{:S(2)}) copy-start(bf16[12288]{0:T(1024)(128)(2,1)} %param.41) | copy-start | bytes 73732
  302.3 23.5 %copy-start.15 = (bf16[3072]{0:T(1024)(128)(2,1)S(1)}, bf16[3072]{0:T(1024)(128)(2,1)}, u32[]{:S(2)}) copy-start(bf16[3072]{0:T(1024)(128)(2,1)} %param.43) | copy-start | bytes 18436
  302.3 24.1 %copy-start.16 = (bf16[3072]{0:T(1024)(128)(2,1)S(1)}, bf16[3072]{0:T(1024)(128)(2,1)}, u32[]{:S(2)}) copy-start(bf16[3072]{0:T(1024)(128)(2,1)} %param.55) | copy-start | bytes 18436
  302.3 24.1 %copy-start.3 = (f32[6,3072]{1,0:T(8,128)S(1)}, f32[6,3072]{1,0:T(8,128)}, u32[]{:S(2)}) copy-start(f32[6,3072]{1,0:T(8,128)} %reshape.36.mi_ref.m_ref) | copy-start | bytes 221188
  302.3 24.1 %copy-start.6 = (bf16[384,3072]{1,0:T(8,128)(2,1)S(1)}, bf16[384,3072]{1,0:T(8,128)(2,1)}, u32[]{:S(2)}) copy-start(bf16[384,3072]{1,0:T(8,128)(2,1)} %get-tuple-element.8.o_ref) | copy-start | bytes 7077892
  325.1 154.1 %all-gather.4.cloned.1.call-start = ((), (), s32[]{:S(2)}) async-start(), calls=%async_computation.2 | async-start | bytes 1671168 | tf_op jit(solution)/shard_map/all_gather | solution.py:642
  326.4 64.0 %slice-start = ((f32[18432]{0:T(1024)}), f32[3072]{0:T(1024)S(1)}, s32[]{:S(2)}) async-start(f32[18432]{0:T(1024)} %copy-done.7), calls=%async_computation.4 | async-start | bytes 24576 | tf_op jit(solution)/shard_map/slice | solution.py:641
  346.9 1.4 copy-start
Sparse Core Ops, SparseCore 0:
  251.5 46.9 all-gather.5
  325.2 65.1 reduce-scatter.1
  393.3 38.5 all-gather.3

commit v2 on v1

--- a/solution.py
+++ b/solution.py
@@ -433,177 +433,246 @@
     )(image, text, m_img, m_txt, w_img, w_txt, b_img, b_txt, g_img, g_txt, cos, se, so)
 
 
-def proj_kernel(o_ref, x_ref, m_ref, w_ref, b_ref, h_ref, z_ref):
-    i = pl.program_id(0)
-    nb = w_ref.shape[1]
-    col = pl.multiple_of(i * nb, nb)
-    sl = pl.ds(col, nb)
-    y = dot(o_ref[...], w_ref[...]) + b_ref[0:1, sl].astype(F32)
-    h_ref[:, sl] = x_ref[:, sl].astype(F32) + m_ref[2:3, sl] * y
-
-    @pl.when(i == pl.num_programs(0) - 1)
-    def _():
+def gelu(x):
+    return x * (0.5 * (1.0 + jnp.tanh(0.7978845608028654 * (x + 0.044715 * (x * x * x)))))
+
+
+def out_kernel(cfg, o_hbm, x_hbm, xt_hbm, ot_ref, mi_ref, mt_ref, wp_hbm, w1_hbm, w2_hbm, twp_hbm, tw1_hbm, tw2_hbm,
+               bp_ref, b1_ref, b2_ref, tbp_ref, tb1_ref, tb2_ref, out_ref, tout_ref,
+               wa, wb, o, x, h, z, acc, a0, a1, o_t, x_t, h_t, z_t, a_t, part, rs, row,
+               asem, bsem, lsem, ossem, orsem, pssem, prsem, rssem, rrsem, fssem, frsem):
+    tok, txt, d, ff, s1, s2 = cfg
+    me = lax.axis_index("cp")
+    chip, core = me // 2, me % 2
+    sib = chip * 2 + (1 - core)
+    rows = txt // 2
+    piece = rows // NCHIP
+    nb = wa.shape[2]
+    na = wa.shape[0]
+    np_ = d // nb
+    nf = ff // nb
+    ft = ff // NCHIP
+    nt = ft // nb
+    nj = ot_ref.shape[0]
+
+    def dev(c):
+        return {"cp": c * 2 + core}
+
+    off = pl.multiple_of(chip * ft, nb)
+    segs_a = ((np_, wp_hbm, 0), (s1, w1_hbm, 0), (np_, twp_hbm, 0), (nt, tw1_hbm, off), (nf - s1, w1_hbm, s1 * nb))
+    segs_b = ((s1, w2_hbm, 0), (nt, tw2_hbm, off), (nf - s1, w2_hbm, s1 * nb))
+
+    def start(p, segs, is_a):
+        lo = 0
+        for n, ref, base in segs:
+            @pl.when((p >= lo) & (p < lo + n))
+            def _(lo=lo, ref=ref, base=base):
+                sl = pl.ds(pl.multiple_of(base + (p - lo) * nb, nb), nb)
+                slot = lax.rem(p, na)
+                if is_a:
+                    pltpu.make_async_copy(ref.at[:, sl], wa.at[slot], asem.at[slot]).start()
+                else:
+                    pltpu.make_async_copy(ref.at[sl, :], wb.at[slot], bsem.at[slot]).start()
+            lo += n
+
+    def get_a(p):
+        start(p + na - 1, segs_a, True)
+        slot = lax.rem(p, na)
+        pltpu.make_async_copy(w1_hbm.at[:, 0:nb], wa.at[slot], asem.at[slot]).wait()
+        return slot
+
+    def get_b(p):
+        start(p + na - 1, segs_b, False)
+        slot = lax.rem(p, na)
+        pltpu.make_async_copy(w2_hbm.at[0:nb, :], wb.at[slot], bsem.at[slot]).wait()
+        return slot
+
+    load_o = pltpu.make_async_copy(o_hbm, o, lsem.at[0])
+    load_x = pltpu.make_async_copy(x_hbm, x, lsem.at[1])
+    load_t = pltpu.make_async_copy(xt_hbm.at[pl.ds(pl.multiple_of(core * rows, 8), rows), :], x_t, lsem.at[2])
+    load_o.start()
+    start(jnp.int32(0), segs_a, True)
+    load_x.start()
+    for p in range(1, na - 1):
+        start(jnp.int32(p), segs_a, True)
+    for p in range(na - 1):
+        start(jnp.int32(p), segs_b, False)
+    load_t.start()
+
+    barrier = pltpu.get_barrier_semaphore()
+    for r in range(1, NCHIP):
+        pl.semaphore_signal(barrier, inc=1, device_id=dev(lax.rem(chip + r, NCHIP)), device_id_type=MESH)
+    pl.semaphore_signal(barrier, inc=1, device_id={"cp": sib}, device_id_type=MESH)
+    pl.semaphore_wait(barrier, NCHIP)
+
+    def o_copy(j, r, c_src, c_dst):
+        return pltpu.make_async_remote_copy(
+            src_ref=ot_ref.at[j], dst_ref=o_t.at[:, pl.ds(pl.multiple_of((j * NCHIP + c_src) * HD, HD), HD)],
+            send_sem=ossem.at[j, r], recv_sem=orsem.at[j, r], device_id=dev(c_dst), device_id_type=MESH)
+
+    for j in range(nj):
+        for r in range(1, NCHIP):
+            o_copy(j, r, chip, lax.rem(chip + r, NCHIP)).start()
+        o_t[:, pl.ds(pl.multiple_of((j * NCHIP + chip) * HD, HD), HD)] = ot_ref[j]
+
+    load_o.wait()
+    load_x.wait()
+
+    def proj(p, carry):
+        slot = get_a(p)
+        sl = pl.ds(pl.multiple_of(p * nb, nb), nb)
+        y = dot(o[...], wa[slot]) + bp_ref[0:1, sl].astype(F32)
+        h[:, sl] = x[:, sl].astype(F32) + mi_ref[2:3, sl] * y
+        return carry
+    lax.fori_loop(0, np_, proj, 0)
+
+    def ln2(src, dst, m_ref, n):
         shift, scale = m_ref[3:4, :], 1.0 + m_ref[4:5, :]
         rb = 16
 
-        def body(k, carry):
-            rows = pl.ds(pl.multiple_of(k * rb, rb), rb)
-            z_ref[rows, :] = ln_mod_rows(h_ref[rows, :], scale, shift).astype(BF16)
+        def body(i, carry):
+            r = pl.ds(pl.multiple_of(i * rb, rb), rb)
+            dst[r, :] = ln_mod_rows(src[r, :], scale, shift).astype(BF16)
             return carry
-        lax.fori_loop(0, h_ref.shape[0] // rb, body, 0)
-
-
-def out_proj(o, x, mods, w, b):
-    tok, d = x.shape
-    nb = 512
-    full = lambda i: (0, 0)
-    return pl.pallas_call(
-        proj_kernel,
-        grid=(d // nb,),
-        out_shape=(jax.ShapeDtypeStruct((tok, d), F32), jax.ShapeDtypeStruct((tok, d), BF16)),
-        in_specs=[pl.BlockSpec((tok, o.shape[1]), full), pl.BlockSpec((tok, d), full), pl.BlockSpec(mods.shape, full),
-                  pl.BlockSpec((w.shape[0], nb), lambda i: (0, i)), pl.BlockSpec(b.shape, full)],
-        out_specs=(pl.BlockSpec((tok, d), full), pl.BlockSpec((tok, d), full)),
-        compiler_params=pltpu.CompilerParams(dimension_semantics=("arbitrary",), vmem_limit_bytes=48 * 2**20),
-        cost_estimate=pl.CostEstimate(flops=2 * tok * d * d, bytes_accessed=2 * d * d, transcendentals=0),
-        name="img_proj",
-    )(o, x, mods, w, b)
-
-
-def gelu(x):
-    return 0.5 * x * (1.0 + jnp.tanh(0.7978845608028654 * (x + 0.044715 * (x * x * x))))
-
-
-def ffn_kernel(last, z_ref, h_ref, m_ref, w1_ref, b1_ref, w2_ref, b2_ref, *rest):
-    i = pl.program_id(0)
-    n = pl.num_programs(0)
-    if last:
-        acc_in, out_ref, acc = rest
-    else:
-        (acc,) = rest
-        acc_in = None
-    a = dot(z_ref[...], w1_ref[...]) + b1_ref[...].astype(F32)
-    a = gelu(a).astype(BF16)
-
-    @pl.when(i == 0)
-    def _():
-        base = b2_ref[...].astype(F32) if acc_in is None else acc_in[...]
-        acc[...] = base + dot(a, w2_ref[...])
-
-    @pl.when(i > 0)
-    def _():
-        acc[...] += dot(a, w2_ref[...])
-
-    if last:
-        @pl.when(i == n - 1)
-        def _():
-            out_ref[...] = (h_ref[...] + m_ref[5:6, :] * acc[...]).astype(BF16)
-
-
-def ffn(z, h, mods, w1, b1, w2, b2, lo, hi, acc_in=None):
-    tok, d = z.shape
+        lax.fori_loop(0, n // rb, body, 0)
+
+    ln2(h, z, mi_ref, tok)
+    acc[...] = jnp.broadcast_to(b2_ref[...].astype(F32), acc.shape)
+
+    def mlp(i, pa, pb, a_new, a_old):
+        slot_b = get_b(pb)
+        slot_a = get_a(pa)
+        sl = pl.ds(pl.multiple_of(i * nb, nb), nb)
+        a_new[...] = gelu(dot(z[...], wa[slot_a]) + b1_ref[0:1, sl].astype(F32)).astype(BF16)
+        acc[...] += dot(a_old[...], wb[slot_b])
+
+    def mlp_range(lo, hi, da, db):
+        def two(k, carry):
+            i = lo + 2 * k
+            mlp(i, i + da, i - 1 + db, a1, a0)
+            mlp(i + 1, i + 1 + da, i + db, a0, a1)
+            return carry
+        lax.fori_loop(0, (hi - lo) // 2, two, 0)
+
+    slot = get_a(jnp.int32(np_))
+    a0[...] = gelu(dot(z[...], wa[slot]) + b1_ref[0:1, 0:nb].astype(F32)).astype(BF16)
+    mlp_range(1, s1, np_, 0)
+    slot = get_b(jnp.int32(s1 - 1))
+    acc[...] += dot(a0[...], wb[slot])
+
+    load_t.wait()
+    for j in range(nj):
+        for r in range(1, NCHIP):
+            o_copy(j, r, lax.rem(chip + NCHIP - r, NCHIP), chip).wait_recv()
+    pa = np_ + s1
+
+    def tproj(k, carry):
+        slot = get_a(pa + k)
+        sl = pl.ds(pl.multiple_of(k * nb, nb), nb)
+        y = dot(o_t[...], wa[slot]) + tbp_ref[0:1, sl].astype(F32)
+        h_t[:, sl] = x_t[:, sl].astype(F32) + mt_ref[2:3, sl] * y
+        return carry
+    lax.fori_loop(0, np_, tproj, 0)
+    ln2(h_t, z_t, mt_ref, rows)
+
+    for k in range(nt):
+        slot = get_a(jnp.int32(pa + np_ + k))
+        y = dot(z_t[...], wa[slot]) + tb1_ref[0:1, pl.ds(pl.multiple_of(off + k * nb, nb), nb)].astype(F32)
+        a_t[:, k * nb:(k + 1) * nb] = gelu(y).astype(BF16)
+    for k in range(nt):
+        slot = get_b(jnp.int32(s1 + k))
+        y = dot(a_t[:, k * nb:(k + 1) * nb], wb[slot])
+        part[...] = y if k == 0 else part[...] + y
+
+    def p_copy(r, c_src, c_dst):
+        return pltpu.make_async_remote_copy(
+            src_ref=part.at[pl.ds(pl.multiple_of(c_dst * piece, 8), piece), :], dst_ref=rs.at[c_src],
+            send_sem=pssem.at[r], recv_sem=prsem.at[r], device_id=dev(c_dst), device_id_type=MESH)
+
+    for r in range(1, NCHIP):
+        p_copy(r, chip, lax.rem(chip + r, NCHIP)).start()
+    mine = pl.ds(pl.multiple_of(chip * piece, 8), piece)
+    rs[chip] = part[mine, :]
+
+    da, db = np_ + np_ + nt, nt
+    slot = get_a(jnp.int32(s1 + da))
+    sl = slice(s1 * nb, (s1 + 1) * nb)
+    a0[...] = gelu(dot(z[...], wa[slot]) + b1_ref[0:1, sl].astype(F32)).astype(BF16)
+    mlp_range(s1 + 1, s2, da, db)
+
+    for r in range(1, NCHIP):
+        p_copy(r, lax.rem(chip + NCHIP - r, NCHIP), chip).wait_recv()
+    tot = rs[0]
+    for c in range(1, NCHIP):
+        tot = tot + rs[c]
+    y = h_t[mine, :] + mt_ref[5:6, :] * (tot + tb2_ref[...].astype(F32))
+    row[...] = y.astype(BF16)
+
+    def r_copy(r, c_src, c_dst):
+        return pltpu.make_async_remote_copy(
+            src_ref=row, dst_ref=tout_ref.at[pl.ds(pl.multiple_of(core * rows + c_src * piece, 8), piece), :],
+            send_sem=rssem.at[r], recv_sem=rrsem.at[r], device_id=dev(c_dst), device_id_type=MESH)
+
+    for r in range(1, NCHIP):
+        r_copy(r, chip, lax.rem(chip + r, NCHIP)).start()
+    tout_ref[pl.ds(pl.multiple_of(core * rows + chip * piece, 8), piece), :] = row[...]
+
+    mlp_range(s2, nf, da, db)
+
+    for r in range(1, NCHIP):
+        r_copy(r, lax.rem(chip + NCHIP - r, NCHIP), chip).wait_recv()
+    ref = tout_ref.at[pl.ds(pl.multiple_of(core * rows, 8), rows), :]
+    fwd = pltpu.make_async_remote_copy(src_ref=ref, dst_ref=ref, send_sem=fssem, recv_sem=frsem,
+                                       device_id={"cp": sib}, device_id_type=MESH)
+    fwd.start()
+
+    slot = get_b(jnp.int32(nf - 1 + db))
+    y = acc[...] + dot((a0 if (nf - 1 - s1) % 2 == 0 else a1)[...], wb[slot])
+    out_ref[...] = (h[...] + mi_ref[5:6, :] * y).astype(BF16)
+
+    fwd.wait()
+    for j in range(nj):
+        for r in range(1, NCHIP):
+            o_copy(j, r, chip, lax.rem(chip + r, NCHIP)).wait_send()
+    for r in range(1, NCHIP):
+        c = lax.rem(chip + r, NCHIP)
+        p_copy(r, chip, c).wait_send()
+        r_copy(r, chip, c).wait_send()
+
+
+def output(o_img, image, text, o_txt, m_img, m_txt, wp, w1, w2, twp, tw1, tw2, *biases):
+    tok, d = image.shape
+    txt = text.shape[0]
     ff = w1.shape[1]
     nb = 512
-    lo, hi = lo // nb, hi // nb
-    full = lambda i: (0, 0)
-    last = acc_in is not None
-    specs = [pl.BlockSpec((tok, d), full), pl.BlockSpec((tok, d), full), pl.BlockSpec(mods.shape, full),
-             pl.BlockSpec((d, nb), lambda i: (0, i + lo)), pl.BlockSpec((1, nb), lambda i: (0, i + lo)),
-             pl.BlockSpec((nb, d), lambda i: (i + lo, 0)), pl.BlockSpec((1, d), full)]
-    args = [z, h, mods, w1, b1, w2, b2]
-    if last:
-        specs.append(pl.BlockSpec((tok, d), full))
-        args.append(acc_in)
+    nf = ff // nb
+    s1 = 3 if nf > 8 else 1
+    s2 = 18 if nf > 8 else 4
+    na = 3
+    rows = txt // 2
+    ft = ff // NCHIP
+    nj = o_txt.shape[0]
+    dma = pltpu.SemaphoreType.DMA
+    flops = 2 * tok * d * (d + 2 * ff) + 2 * rows * d * (d + 2 * ft)
     return pl.pallas_call(
-        functools.partial(ffn_kernel, last),
-        grid=(hi - lo,),
-        out_shape=jax.ShapeDtypeStruct((tok, d), BF16 if last else F32),
-        in_specs=specs,
-        out_specs=pl.BlockSpec((tok, d), full),
-        scratch_shapes=[pltpu.VMEM((tok, d), F32)] if last else [],
-        compiler_params=pltpu.CompilerParams(dimension_semantics=("arbitrary",), vmem_limit_bytes=VMEM_LIMIT),
-        cost_estimate=pl.CostEstimate(flops=4 * tok * d * (hi - lo) * nb, bytes_accessed=4 * d * (hi - lo) * nb,
-                                      transcendentals=tok * (hi - lo) * nb),
-        name="img_ffn",
-    )(*args)
-
-
-def txt_kernel(og_ref, x_ref, m_ref, wp_hbm, bp_ref, w1_hbm, b1_ref, w2_hbm, h_ref, part_ref,
-               o, h, wp, w1, w2, z, a, sem, psem):
-    me = lax.axis_index("cp")
-    txt, d = x_ref.shape
-    fb = w1.shape[1]
-    nj = og_ref.shape[1]
-    nb = wp.shape[2]
-    c1 = pltpu.make_async_copy(w1_hbm.at[:, pl.ds(pl.multiple_of(me * fb, 128), fb)], w1, sem.at[0])
-    c2 = pltpu.make_async_copy(w2_hbm.at[pl.ds(pl.multiple_of(me * fb, 128), fb), :], w2, sem.at[1])
-
-    def cp(i, slot):
-        return pltpu.make_async_copy(wp_hbm.at[:, pl.ds(pl.multiple_of(i * nb, nb), nb)], wp.at[slot], psem.at[slot])
-
-    nstep = d // nb
-    cp(0, 0).start()
-    c1.start()
-    c2.start()
-    rows = txt // 2
-    for c in range(NCHIP):
-        for k in range(2):
-            for j in range(nj):
-                o[k * rows:(k + 1) * rows, (j * NCHIP + c) * HD:(j * NCHIP + c + 1) * HD] = og_ref[c * 2 + k, j]
-
-    def body(i, carry):
-        slot = lax.rem(i, 2)
-
-        @pl.when(i + 1 < nstep)
-        def _():
-            cp(i + 1, 1 - slot).start()
-        cp(i, slot).wait()
-        sl = pl.ds(pl.multiple_of(i * nb, nb), nb)
-        y = dot(o[...], wp[slot]) + bp_ref[0:1, sl].astype(F32)
-        h[:, sl] = x_ref[:, sl].astype(F32) + m_ref[2:3, sl] * y
-        return carry
-    lax.fori_loop(0, nstep, body, 0)
-    shift, scale = m_ref[3:4, :], 1.0 + m_ref[4:5, :]
-    rb = 16
-
-    def lnb(k, carry):
-        r = pl.ds(pl.multiple_of(k * rb, rb), rb)
-        z[r, :] = ln_mod_rows(h[r, :], scale, shift).astype(BF16)
-        return carry
-    lax.fori_loop(0, txt // rb, lnb, 0)
-    h_ref[...] = h[pl.ds(pl.multiple_of(me * (txt // NDEV), 8), txt // NDEV), :]
-    c1.wait()
-    y = dot(z[...], w1[...]) + b1_ref[0:1, pl.ds(pl.multiple_of(me * fb, 128), fb)].astype(F32)
-    a[...] = gelu(y).astype(BF16)
-    c2.wait()
-
-    def fc2(i, carry):
-        sl = pl.ds(pl.multiple_of(i * nb, nb), nb)
-        part_ref[:, sl] = dot(a[...], w2[:, sl])
-        return carry
-    lax.fori_loop(0, nstep, fc2, 0)
-
-
-def text_mlp(og, x, mods, wp, bp, w1, b1, w2):
-    txt, d = x.shape
-    ff = w1.shape[1]
-    fb = ff // NDEV
-    nb = 512
-    dma = pltpu.SemaphoreType.DMA
-    return pl.pallas_call(
-        txt_kernel,
-        out_shape=(jax.ShapeDtypeStruct((txt // NDEV, d), F32), jax.ShapeDtypeStruct((txt, d), F32)),
-        in_specs=[VM, VM, VM, ANY, VM, ANY, VM, ANY],
+        functools.partial(out_kernel, (tok, txt, d, ff, s1, s2)),
+        out_shape=(jax.ShapeDtypeStruct((tok, d), BF16), jax.ShapeDtypeStruct((txt, d), BF16)),
+        in_specs=[ANY, ANY, ANY, VM, VM, VM] + [ANY] * 6 + [VM] * 6,
         out_specs=(VM, VM),
         scratch_shapes=[
-            pltpu.VMEM((txt, wp.shape[0]), BF16), pltpu.VMEM((txt, d), F32), pltpu.VMEM((2, wp.shape[0], nb), BF16),
-            pltpu.VMEM((d, fb), BF16), pltpu.VMEM((fb, d), BF16), pltpu.VMEM((txt, d), BF16), pltpu.VMEM((txt, fb), BF16),
-            dma((2,)), dma((2,)),
+            pltpu.VMEM((na, d, nb), BF16), pltpu.VMEM((na, nb, d), BF16),
+            pltpu.VMEM((tok, d), BF16), pltpu.VMEM((tok, d), BF16), pltpu.VMEM((tok, d), F32), pltpu.VMEM((tok, d), BF16),
+            pltpu.VMEM((tok, d), F32), pltpu.VMEM((tok, nb), BF16), pltpu.VMEM((tok, nb), BF16),
+            pltpu.VMEM((rows, d), BF16), pltpu.VMEM((rows, d), BF16), pltpu.VMEM((rows, d), F32), pltpu.VMEM((rows, d), BF16),
+            pltpu.VMEM((rows, ft), BF16), pltpu.VMEM((rows, d), F32), pltpu.VMEM((NCHIP, rows // NCHIP, d), F32),
+            pltpu.VMEM((rows // NCHIP, d), BF16),
+            dma((na,)), dma((na,)), dma((3,)), dma((nj, NCHIP)), dma((nj, NCHIP)), dma((NCHIP,)), dma((NCHIP,)),
+            dma((NCHIP,)), dma((NCHIP,)), dma, dma,
         ],
-        compiler_params=pltpu.CompilerParams(vmem_limit_bytes=48 * 2**20),
-        cost_estimate=pl.CostEstimate(flops=2 * txt * d * (d + 2 * fb), bytes_accessed=2 * d * (d + 2 * fb), transcendentals=0),
-        name="txt_mlp",
-    )(og, x, mods, wp, bp, w1, b1, w2)
+        compiler_params=pltpu.CompilerParams(collective_id=2, has_side_effects=True, vmem_limit_bytes=VMEM_LIMIT),
+        cost_estimate=pl.CostEstimate(flops=flops, bytes_accessed=2 * d * (d + 2 * ff), transcendentals=0),
+        name="out",
+    )(o_img, image, text, o_txt, m_img, m_txt, wp, w1, w2, twp, tw1, tw2, *biases)
 
 
 def rope_tables(ids):
@@ -632,15 +701,8 @@
     cos, se, so = rope_tables(image_ids)
     o_img, o_txt = attention(x, xt, m_img, m_txt, wqkv, twqkv, row(bqkv), row(tbqkv),
                              jnp.stack([qg, kg]), jnp.stack([tqg, tkg]), cos, se, so)
-    og = lax.all_gather(o_txt, "cp")
-    h, z = out_proj(o_img, x, m_img, wp, row(bp))
-    ht, part = text_mlp(og, xt, m_txt, twp, row(tbp), tw1, row(tb1), tw2)
-    ff = w1.shape[1]
-    acc = ffn(z, h, m_img, w1, row(b1), w2, row(b2), 0, ff // 2)
-    red = lax.psum_scatter(part, "cp", scatter_dimension=0, tiled=True)
-    rows = (ht + m_txt[5:6] * (red + tb2.astype(F32)[None, :])).astype(BF16)
-    text_out = lax.all_gather(rows, "cp", tiled=True)
-    image_out = ffn(z, h, m_img, w1, row(b1), w2, row(b2), ff // 2, ff, acc)
+    image_out, text_out = output(o_img, x, xt, o_txt, m_img, m_txt, wp, w1, w2, twp, tw1, tw2,
+                                 row(bp), row(b1), row(b2), row(tbp), row(tb1), row(tb2))
     return image_out[None], text_out[None]
 
 

time: 492 us -> 376 us (0.76)
  waiting for transfers between devices: 87.6 us -> 0 us
  Pallas kernels: 368 us -> 348 us
  between operations: 14.5 us -> 0.94 us
    all_gather x2 -> x0, waiting for transfers between devices: 45.4 us -> none  [the longest x1 45.4 us: device_fn(): og = lax.all_gather(o_txt, 'cp')]
    reduce_scatter x1 -> x0, waiting for transfers between devices: 42.1 us -> none  [device_fn(): red = lax.psum_scatter(part, 'cp', scatter_dimension=0, tiled=True)]
    pallas_call x4 -> x1, Pallas kernels: 130 us -> 110 us  [output(): pl.pallas_call(functools.partial(out_kernel, (tok, txt, d, ff, s1, s2)),...]
    broadcast_in_dim x7 -> x8, local copies, waits for them, and re-layouts: 3.99 us -> 10.6 us  [device_fn(): row = lambda v: v[None, :]]
  transfers between devices with their start and end apart: 3 -> 0, of which waited for: 2 -> 0; matrix products, arithmetic and copies ran while one was open for 1% -> 0% of each run, Pallas kernels for 22% -> 0%
where the time goes in v2:
time: 376 us; the launch traced here: 372 us
  Pallas kernels  348 us (93%)
  local copies, waits for them, and re-layouts  18.9 us (5%)
  other arithmetic  3.96 us (1%)
    pallas_call x1, Pallas kernels, attention(): pl.pallas_call(functools.partial(main_kernel, cfg), out_shape=(jax.ShapeD...  224 us
    pallas_call x1, Pallas kernels, output(): pl.pallas_call(functools.partial(out_kernel, (tok, txt, d, ff, s1, s2)),...  110 us
    pallas_call x1, Pallas kernels, modulation(): pl.pallas_call(mod_kernel, out_shape=jax.ShapeDtypeStruct((NDEV, pad, 128...  14.5 us
    broadcast_in_dim x8, local copies, waits for them, and re-layouts, device_fn(): row = lambda v: v[None, :]  10.6 us

profile of v2, /device:TPU:0, one launch (start us, length us, event | category | flops | bytes accessed | tf_op | source)
XLA Modules:
  0.0 372.2 jit_solution(15264157183087898579)
XLA Ops:
  0.7 1.3 pad_maximum_fusion.1
  2.0 0.1 broadcast_in_dim.42
  2.1 0.1 mul.79
  2.1 0.7 convert_element_type.23
  2.9 1.3 broadcast_in_dim.44.bp_ref
  4.2 1.3 broadcast_in_dim.46.b2_ref
  5.5 1.3 broadcast_in_dim.47.tbp_ref
  6.8 1.3 broadcast_in_dim.49.tb2_ref
  8.1 0.1 broadcast_in_dim.43
  8.1 0.1 mul.85
  8.2 1.4 broadcast_in_dim.40.bi_ref
  9.6 1.4 broadcast_in_dim.41.bt_ref
  10.9 1.4 broadcast_in_dim.45.b1_ref
  12.3 1.4 broadcast_in_dim.48.tb1_ref
  13.7 0.1 broadcast_multiply_fusion.3
  13.8 0.0 copy-start
  13.8 0.7 copy-done
  14.5 0.0 copy-start.1
  14.5 0.0 copy-start.2
  14.5 14.5 %mod.1 = f32[16,24,128]{2,1,0:T(8,128)S(1)} custom-call(bf16[1,3072]{1,0:T(2,128)(2,1)S(1)} %copy-done, bf16[3072,18432]{1,0:T(8,128)(2,1)} %wi_hbm.2, bf16[3072,18432]{1,0:T(8,128)(2,1)} %wt_hbm.2), custom_call_target="tpu_custom_call" | custom-call | flops 226492416 | bytes 14155776 | tf_op jit(solution)/shard_map/mod/pallas_call | solution.py:75
  29.1 0.0 copy-done.1
  29.1 0.6 reshape.35.mt_ref
  29.8 0.0 copy-done.2
  29.8 0.6 reshape.33.mi_ref
  30.4 0.2 broadcast_multiply_fusion.2
  30.6 1.6 broadcast_multiply_fusion
  32.2 223.5 %attn.1 = (bf16[384,3072]{1,0:T(8,128)(2,1)}, bf16[3,128,128]{2,1,0:T(8,128)(2,1)}) custom-call(bf16[384,3072]{1,0:T(8,128)(2,1)} %bitcast.8, bf16[256,3072]{1,0:T(8,128)(2,1)} %bitcast.11, f32[6,3072]{1,0:T(8,128)} %reshape.33.mi_ref, f32[6,3072]{1,0:T(8,128)} %reshape.35.mt_ref, bf16[3072,9216]{1,0:T(8,128)(2,1)} %wi_hbm.3, bf16[3072,9216]{1,0:T(8,128)(2,1)} %wt_hbm.3, ...), custom_call_target="tpu_custom_call" | custom-call | flops 54458843136 | bytes 56623104 | tf_op jit(solution)/shard_map/attn/pallas_call | solution.py:407
  255.8 110.4 %out.1 = (bf16[384,3072]{1,0:T(8,128)(2,1)}, bf16[256,3072]{1,0:T(8,128)(2,1)}) custom-call(bf16[384,3072]{1,0:T(8,128)(2,1)} %get-tuple-element.6.o_hbm, bf16[384,3072]{1,0:T(8,128)(2,1)} %bitcast.9, bf16[256,3072]{1,0:T(8,128)(2,1)} %bitcast.12, bf16[3,128,128]{2,1,0:T(8,128)(2,1)} %get-tuple-element.7.ot_ref, f32[6,3072]{1,0:T(8,128)} %reshape.33.mi_ref, ...), custom_call_target="tpu_custom_call" | custom-call | flops 70061654016 | bytes 169869312 | tf_op jit(solution)/shard_map/out/pallas_call | solution.py:657
  366.2 3.2 copy.32
  369.4 2.7 copy.33
  (10 shorter events, 0.1 us)
Async XLA Ops:
  13.8 0.7 copy-start
  14.5 14.6 %copy-start.1 = (bf16[18432]{0:T(1024)(128)(2,1)S(1)}, bf16[18432]{0:T(1024)(128)(2,1)}, u32[]{:S(2)}) copy-start(bf16[18432]{0:T(1024)(128)(2,1)} %param.45) | copy-start | bytes 110596
  14.5 15.2 %copy-start.2 = (bf16[18432]{0:T(1024)(128)(2,1)S(1)}, bf16[18432]{0:T(1024)(128)(2,1)}, u32[]{:S(2)}) copy-start(bf16[18432]{0:T(1024)(128)(2,1)} %param.33) | copy-start | bytes 110596

commit v3 on v2

v3 whole, which is shorter than its diff:
```python
import functools

import jax
import jax.numpy as jnp
from jax import lax
from jax.experimental import pallas as pl
from jax.experimental.pallas import tpu as pltpu
from jax.sharding import PartitionSpec as P

EPS = 1e-6
THETA = 10000.0
F32 = jnp.float32
BF16 = jnp.bfloat16
HD = 128
NCHIP = 8
NDEV = 16
VM = pl.BlockSpec(memory_space=pltpu.VMEM)
ANY = pl.BlockSpec(memory_space=pl.ANY)
MESH = pl.DeviceIdType.MESH
VMEM_LIMIT = 67043328


def dot(a, b):
    return jnp.dot(a, b, preferred_element_type=F32)


def dot_t(a, b):
    return lax.dot_general(a, b, (((1,), (1,)), ((), ())), preferred_element_type=F32)


def bias_row(b_ref, row, n):
    return jnp.concatenate([b_ref[pl.ds(row + i, 1), :] for i in range(n)], axis=1)


def ln_mod_rows(x, scale1p, shift):
    xf = x.astype(F32)
    mean = jnp.mean(xf, axis=-1, keepdims=True)
    cent = xf - mean
    var = jnp.mean(cent * cent, axis=-1, keepdims=True)
    return scale1p * (cent * lax.rsqrt(var + EPS)) + shift


def main_kernel(cfg, boff, x_hbm, xt_hbm, cond_ref, wmi_hbm, wmt_hbm, wi_hbm, wt_hbm, b_ref, g_ref, pos_ref, om_ref,
                o_hbm, ot_ref, g2,
                xs, xm, xt, ks, vs, qs, kb, vb, qb, posm, cos_t, se_t, so_t, mi, mt, g1, mine1, mine2,
                xsem, wsem, wxsem, msend, mrecv, gsend, grecv, ssem, rsem, fssem, frsem, ossem, orsem):
    tok, txt, d_in, heads, ck = cfg
    hd_all = heads * HD
    nj = heads // NCHIP
    quad = 4
    me = lax.axis_index("cp")
    chip, core = me // 2, me % 2
    zh, cl = chip // quad, chip % quad
    plane = cl // 2
    sib = chip * 2 + (1 - core)
    mirror = lax.rem(chip + quad, NCHIP) * 2 + core
    outer = ((chip // 2) == 0) | ((chip // 2) == 3)
    m1 = 2 * tok // 3
    m2 = tok - m1
    sizes = (tok, m1, m2)
    rows0 = (0, tok, tok + m1)
    qpos = (txt, txt + quad * tok, txt + quad * (tok + m1))
    kpos = (txt, txt + 2 * quad * tok, txt + 2 * quad * (tok + m1))

    def same(c_local):
        return {"cp": (zh * quad + c_local) * 2 + core}

    def dev(c):
        return {"cp": c * 2 + core}

    barrier = pltpu.get_barrier_semaphore()
    for r in range(1, NDEV):
        pl.semaphore_signal(barrier, inc=1, device_id={"cp": lax.rem(me + r, NDEV)}, device_id_type=MESH)
    load_x = pltpu.make_async_copy(x_hbm, xs, xsem.at[0])
    load_t = pltpu.make_async_copy(xt_hbm, xt, xsem.at[1])

    def x_copy(part):
        sl = pl.ds(0, m1) if part == 0 else pl.ds(m1, m2)
        return pltpu.make_async_remote_copy(
            src_ref=x_hbm.at[sl, :], dst_ref=xm.at[sl, :], send_sem=msend.at[part], recv_sem=mrecv.at[part],
            device_id={"cp": mirror}, device_id_type=MESH)

    pos_copy = pltpu.make_async_remote_copy(
        src_ref=pos_ref, dst_ref=posm, send_sem=msend.at[2], recv_sem=mrecv.at[2],
        device_id={"cp": mirror}, device_id_type=MESH)

    def qkv_phase(w, wx):
        wide = quad * HD
        wc = wx.shape[2]
        kinds = (1, 2, 0)

        def w_copy(n):
            j, kind = n // 3, kinds[n % 3]
            off = pl.multiple_of(kind * hd_all + j * NCHIP * HD + zh * wide, wide)
            return pltpu.make_async_copy(wi_hbm.at[:, pl.ds(off, wide)], w.at[n], wsem.at[n])

        first = 2 * d_in // NDEV
        rest = 4 * d_in // NDEV
        n1, n2 = first // wc, rest // wc
        side = [(r, i) for r in ("mi1", "mt1") for i in range(n1)] + [("t", kind) for kind in kinds]
        side += [(r, i) for r in ("mi2", "mt2") for i in range(n2)]
        nslot = wx.shape[0]

        def side_copies(n):
            what, i = side[n]
            slot = n % nslot
            if what == "t":
                return [pltpu.make_async_copy(
                    wt_hbm.at[:, pl.ds(pl.multiple_of(i * hd_all + (j * NCHIP + chip) * HD, HD), HD)],
                    wx.at[slot, :, pl.ds(j * HD, HD)], wxsem.at[slot, j]) for j in range(nj)]
            ref = wmi_hbm if what[:2] == "mi" else wmt_hbm
            off = me * first + i * wc if what[2] == "1" else 2 * d_in + me * rest + i * wc
            return [pltpu.make_async_copy(ref.at[:, pl.ds(pl.multiple_of(off, 128), wc)], wx.at[slot], wxsem.at[slot, 0])]

        def side_start(n):
            if n < len(side):
                for c in side_copies(n):
                    c.start()

        def side_get(n):
            side_start(n + nslot - 1)
            for c in side_copies(n):
                c.wait()
            return n % nslot

        for n in range(nslot - 1):
            side_start(n)
        load_x.start()
        for n in range(3 * nj):
            w_copy(n).start()
        load_t.start()

        c = cond_ref[...].astype(F32)
        act = (c * jax.nn.sigmoid(c)).astype(BF16)
        act = jnp.broadcast_to(act, (16, d_in))
        pl.semaphore_wait(barrier, NDEV - 1)

        @pl.when(jnp.logical_not(outer))
        def _():
            x_copy(0).start()
            x_copy(1).start()
        pos_copy.start()

        per = wc // 128

        def mod_rows(n, buf, row):
            r = dot(act, wx[side_get(n)])
            for i in range(per):
                buf[row + i:row + i + 1, :] = r[0:1, i * 128:(i + 1) * 128]

        def spread(buf, dst, k):
            return [pltpu.make_async_remote_copy(
                src_ref=buf, dst_ref=dst.at[me], send_sem=gsend.at[k, r], recv_sem=grecv.at[k, r],
                device_id={"cp": lax.rem(me + r, NDEV)}, device_id_type=MESH) for r in range(1, NDEV)]

        mine1[...] = jnp.zeros_like(mine1)
        for n in range(2 * n1):
            mod_rows(n, mine1, n * per)
        gath1 = spread(mine1, g1, 0)
        for cp in gath1:
            cp.start()
        g1[me] = mine1[...]

        def tables(pos):
            ang = pos.astype(F32) * om_ref[...]
            odd = lax.rem(lax.broadcasted_iota(jnp.int32, ang.shape, 1), 2) == 1
            sin = jnp.sin(ang)
            cos_t[...] = jnp.cos(ang)
            se_t[...] = jnp.where(odd, 0.0, -sin)
            so_t[...] = jnp.where(odd, sin, 0.0)

        tables(pos_ref[...])
        for cp in gath1:
            cp.wait()
        rows1 = n1 * per
        for b, m in ((0, mi), (1, mt)):
            for dv in range(NDEV):
                for r in range(rows1):
                    col = (dv * rows1 + r) * 128
                    v = g1[dv, b * rows1 + r:b * rows1 + r + 1, :] + b_ref[boff[b] + dv * rows1 + r:boff[b] + dv * rows1 + r + 1, :]
                    m[col // d_in:col // d_in + 1, col % d_in:col % d_in + 128] = v

        rb = 16

        def ln_rows(ref, m_ref, lo, n):
            shift = m_ref[0:1, :]
            scale = 1.0 + m_ref[1:2, :]

            def body(i, carry):
                sl = pl.ds(pl.multiple_of(lo + i * rb, rb), rb)
                ref[sl, :] = ln_mod_rows(ref[sl, :], scale, shift).astype(BF16)
                return carry
            lax.fori_loop(0, n // rb, body, 0)

        def norm_rope(y, gain, lo, n):
            ms = jnp.mean(y * y, axis=-1, keepdims=True)
            y = y * lax.rsqrt(ms + EPS) * gain
            if lo is not None:
                sl = slice(lo, lo + n)
                y = y * cos_t[sl, :] + pltpu.roll(y, HD - 1, 1) * se_t[sl, :] + pltpu.roll(y, 1, 1) * so_t[sl, :]
            return y

        def qkv_copy(kind, st, j, c_src, c_dst, sem_i):
            n = sizes[st]
            src, dst = ((qs, qb), (ks, kb), (vs, vb))[kind]
            lo = rows0[st]
            if kind == 0:
                s, t = src.at[j * quad + c_dst, pl.ds(lo, n)], dst.at[j, pl.ds(pl.multiple_of(qpos[st] + c_src * n, 128), n)]
            else:
                at = pl.multiple_of(kpos[st] + core * quad * n + c_src * n, 128)
                if kind == 1:
                    s, t = src.at[j * quad + c_dst, pl.ds(lo, n)], dst.at[j, pl.ds(at, n)]
                else:
                    s, t = src.at[j * quad + c_dst, :, pl.ds(lo, n)], dst.at[j, :, pl.ds(at, n)]
            return pltpu.make_async_remote_copy(
                src_ref=s, dst_ref=t, send_sem=ssem.at[kind, st, j, sem_i], recv_sem=rsem.at[kind, st, j, sem_i],
                device_id=same(c_dst), device_id_type=MESH)

        def own_copy(kind, st, j):
            n, lo = sizes[st], rows0[st]
            h = j * quad + cl
            if kind == 0:
                qb[j, pl.ds(pl.multiple_of(qpos[st] + cl * n, 128), n)] = qs[h, lo:lo + n]
            else:
                at = pl.multiple_of(kpos[st] + core * quad * n + cl * n, 128)
                if kind == 1:
                    kb[j, pl.ds(at, n)] = ks[h, lo:lo + n]
                else:
                    vb[j, :, pl.ds(at, n)] = vs[h, :, lo:lo + n]

        def qkv_set(st, src, src_lo, tab_lo):
            n, lo = sizes[st], rows0[st]

            def per_j(j, carry):
                for i, kind in enumerate(kinds):
                    tile = 3 * j + i
                    if st == 0:
                        pltpu.make_async_copy(wi_hbm.at[:, 0:wide], w.at[tile], wsem.at[tile]).wait()

                    def cols(p, carry):
                        col = pl.multiple_of(p * 2 * HD, 2 * HD)
                        y2 = dot(src[src_lo:src_lo + n, :], w[tile, :, pl.ds(col, 2 * HD)])
                        for hh in range(2):
                            h = 2 * p + hh
                            brow = boff[2] + kind * heads + j * NCHIP + zh * quad + h
                            y = y2[:, hh * HD:(hh + 1) * HD] + b_ref[pl.ds(brow, 1), :]
                            head = j * quad + h
                            if kind == 2:
                                vs[head, :, lo:lo + n] = y.T.astype(BF16)
                            else:
                                y = norm_rope(y, g_ref[kind:kind + 1, :], tab_lo, n).astype(BF16)
                                (qs, ks)[kind][head, lo:lo + n] = y
                        return carry
                    lax.fori_loop(0, 2, cols, 0)
                    own_copy(kind, st, j)
                    for r in range(1, quad):
                        qkv_copy(kind, st, j, cl, lax.rem(cl + r, quad), r).start()
                return carry
            lax.fori_loop(0, nj, per_j, 0)

        def arrived(kind, st, j):
            for r in range(1, quad):
                qkv_copy(kind, st, j, lax.rem(cl + quad - r, quad), cl, r).wait_recv()

        load_x.wait()
        ln_rows(xs, mi, 0, tok)
        qkv_set(0, xs, 0, 0)

        @pl.when(outer)
        def _():
            x_copy(0).start()
            x_copy(1).start()

        load_t.wait()
        ln_rows(xt, mt, 0, txt)
        for i, kind in enumerate(kinds):
            slot = side_get(2 * n1 + i)
            y3 = dot(xt[...], wx[slot, :, 0:nj * HD])
            for j in range(nj):
                brow = boff[3] + kind * heads + j * NCHIP + chip
                y = y3[:, j * HD:(j + 1) * HD] + b_ref[pl.ds(brow, 1), :]
                if kind == 2:
                    vb[j, :, 0:txt] = y.T.astype(BF16)
                else:
                    (qb, kb)[kind][j, 0:txt] = norm_rope(y, g_ref[2 + kind:3 + kind, :], None, txt).astype(BF16)

        mine2[...] = jnp.zeros_like(mine2)
        for n in range(2 * n2):
            mod_rows(2 * n1 + 3 + n, mine2, n * per)
        gath2 = spread(mine2, g2, 1)
        for cp in gath2:
            cp.start()
        g2[me] = mine2[...]

        pos_copy.wait_recv()
        tables(posm[...])
        x_copy(0).wait_recv()
        ln_rows(xm, mi, 0, m1)
        qkv_set(1, xm, 0, 0)

        def to_sibling(kind, st, j):
            n = quad * sizes[st]
            at = pl.multiple_of(kpos[st] + core * n, 128)
            ref = kb.at[j, pl.ds(at, n)] if kind == 1 else vb.at[j, :, pl.ds(at, n)]
            return pltpu.make_async_remote_copy(
                src_ref=ref, dst_ref=ref, send_sem=fssem.at[kind - 1, st, j], recv_sem=frsem.at[kind - 1, st, j],
                device_id={"cp": sib}, device_id_type=MESH)

        for j in range(nj):
            for kind in (1, 2):
                arrived(kind, 0, j)
                to_sibling(kind, 0, j).start()
            arrived(0, 0, j)
        x_copy(1).wait_recv()
        ln_rows(xm, mi, m1, m2)
        qkv_set(2, xm, m1, m1)
        for j in range(nj):
            for kind in (1, 2):
                arrived(kind, 1, j)
                to_sibling(kind, 1, j).start()
            arrived(0, 1, j)
        for j in range(nj):
            for kind in (1, 2):
                arrived(kind, 2, j)
                to_sibling(kind, 2, j).start()
            arrived(0, 2, j)

        for cp in gath2:
            cp.wait()
        for part in range(2):
            x_copy(part).wait_send()
        pos_copy.wait_send()
        for j in range(nj):
            for st in range(3):
                for kind in range(3):
                    for r in range(1, quad):
                        qkv_copy(kind, st, j, cl, lax.rem(cl + r, quad), r).wait_send()
                for kind in (1, 2):
                    to_sibling(kind, st, j).wait()

    pl.run_scoped(qkv_phase, pltpu.VMEM((3 * nj, d_in, quad * HD), BF16), pltpu.VMEM((3, d_in, 2 * d_in // NDEV), BF16))

    scale2 = (HD ** -0.5) * 1.4426950408889634
    qt = 256
    keys = txt + 2 * quad * 2 * tok
    nchunk = keys // ck
    n_own, n_m1, n_m2 = quad * tok // qt, quad * m1 // qt, quad * m2 // qt
    ntile = 1 + n_own + n_m1 + n_m2
    g = n_own // 2

    def attention_phase(s0, s1, mx0, mx1, ost, otmp):
        def tile_start(t):
            own = t - 1 - n_m1 - n_m2
            p = jnp.where(own < g, 1 - plane, plane)
            row_own = txt + p * (2 * tok) + lax.rem(own + 2 * g, g) * qt
            row_mir = txt + quad * tok + (t - 1) * qt
            return pl.multiple_of(jnp.where(t == 0, 0, jnp.where(own < 0, row_mir, row_own)), 128)

        def qk(j, q, i, s_ref, mx):
            sl = pl.ds(pl.multiple_of(i * ck, ck), ck)
            s = dot_t(kb[j, sl], q)
            s_ref[sl, :] = s
            return jnp.maximum(mx, jnp.max(s.reshape(ck // 8, 8, qt), axis=0))

        def sm(j, i, s_ref, m, lsum, acc):
            sl = pl.ds(pl.multiple_of(i * ck, ck), ck)
            p = jnp.exp2((s_ref[sl, :] - m) * scale2)
            lsum = lsum + jnp.sum(p.reshape(ck // 8, 8, qt), axis=0)
            acc = acc + dot(vb[j, :, sl], p.astype(BF16))
            return lsum, acc

        def new_max():
            return jnp.full((8, qt), -jnp.inf, F32)

        def o_copy(j, c_src, c_dst, st):
            n = sizes[st]
            cd = lax.rem(c_dst, quad)
            base = (0, quad * tok, quad * (tok + m1))[st]
            dst_row = (0, 0, m1)[st]
            src = ost.at[j, pl.ds(pl.multiple_of(base + cd * n, 128), n)]
            dst = o_hbm.at[pl.ds(dst_row, n), pl.ds(pl.multiple_of((j * NCHIP + c_src) * HD, HD), HD)]
            return src, dst, dict(send_sem=ossem.at[j, st, cd], recv_sem=orsem.at[j, c_src, 1 if st == 2 else 0],
                                  device_id=dev(c_dst), device_id_type=MESH)

        def o_remote(j, c_src, c_dst, st):
            src, dst, kw = o_copy(j, c_src, c_dst, st)
            return pltpu.make_async_remote_copy(src_ref=src, dst_ref=dst, **kw)

        def o_local(j):
            src, dst, kw = o_copy(j, chip, chip, 0)
            return pltpu.make_async_copy(src, dst, kw["send_sem"])

        def send_own(j, p):
            for y in range(2):
                c = zh * quad + p * 2 + y

                @pl.when(c != chip)
                def _():
                    o_remote(j, chip, c, 0).start()

                @pl.when(c == chip)
                def _():
                    o_local(j).start()

        def finish(j, t, lsum, acc):
            tot = jnp.sum(lsum, axis=0, keepdims=True)
            o = (acc / tot).T.astype(BF16)

            @pl.when(t == 0)
            def _():
                otmp[...] = o
                ot_ref[j] = otmp[pl.ds(pl.multiple_of(core * (txt // 2), 8), txt // 2), :]

            @pl.when(t > 0)
            def _():
                ost[j, pl.ds(pl.multiple_of(tile_start(t) - txt, 128), qt)] = o

            far = (1 - zh) * quad

            @pl.when((t > 0) & (t <= n_m1))
            def _():
                o_remote(j, chip, far + t - 1, 1).start()

            @pl.when((t > n_m1) & (t <= n_m1 + n_m2))
            def _():
                for y in range(2):
                    o_remote(j, chip, far + 2 * (t - 1 - n_m1) + y, 2).start()

            @pl.when(t == n_m1 + n_m2 + g)
            def _():
                send_own(j, 1 - plane)

            @pl.when(t == n_m1 + n_m2 + 2 * g)
            def _():
                send_own(j, plane)

        def pair(j, t, s_cur, mx_cur, s_nxt, mx_nxt, has_next):
            m = jnp.max(mx_cur[...], axis=0, keepdims=True)
            lsum = jnp.zeros((8, qt), F32)
            acc = jnp.zeros((HD, qt), F32)
            if has_next:
                q = qb[j, pl.ds(tile_start(t + 1), qt)]

                def body(i, carry):
                    lsum, acc, mx = carry
                    mx = qk(j, q, i, s_nxt, mx)
                    lsum, acc = sm(j, i, s_cur, m, lsum, acc)
                    return lsum, acc, mx
                lsum, acc, mx = lax.fori_loop(0, nchunk, body, (lsum, acc, new_max()))
                mx_nxt[...] = mx
            else:
                def body(i, carry):
                    return sm(j, i, s_cur, m, *carry)
                lsum, acc = lax.fori_loop(0, nchunk, body, (lsum, acc))
            finish(j, t, lsum, acc)

        def head(j, carry):
            q = qb[j, 0:qt]

            def first(i, mx):
                return qk(j, q, i, s0, mx)
            mx0[...] = lax.fori_loop(0, nchunk, first, new_max())

            def two(i, carry):
                pair(j, 2 * i, s0, mx0, s1, mx1, True)
                pair(j, 2 * i + 1, s1, mx1, s0, mx0, True)
                return carry
            lax.fori_loop(0, (ntile - 1) // 2, two, 0)
            pair(j, jnp.int32(ntile - 1), s0, mx0, s1, mx1, False)
            return carry
        lax.fori_loop(0, nj, head, 0)

        for j in range(nj):
            o_local(j).wait()
            for r in range(1, quad):
                c = zh * quad + lax.rem(cl + r, quad)
                o_remote(j, chip, c, 0).wait_send()
                o_remote(j, c, chip, 0).wait_recv()
            for r in range(quad):
                c = (1 - zh) * quad + r
                for st in (1, 2):
                    o_remote(j, chip, c, st).wait_send()
                    o_remote(j, c, chip, st).wait_recv()

    pl.run_scoped(attention_phase, pltpu.VMEM((keys, qt), F32), pltpu.VMEM((keys, qt), F32), pltpu.VMEM((8, qt), F32),
                  pltpu.VMEM((8, qt), F32), pltpu.VMEM((nj, 2 * quad * tok, HD), BF16), pltpu.VMEM((txt, HD), BF16))


def attention(image, text, cond_vec, wm_img, wm_txt, w_img, w_txt, biases, boff, gains, pos, omega):
    tok, d_in = image.shape
    txt = text.shape[0]
    hd_all = w_img.shape[1] // 3
    heads = hd_all // HD
    nj = heads // NCHIP
    half = tok * NCHIP
    keys = txt + 2 * half
    ck = 1280
    cfg = (tok, txt, d_in, heads, ck)
    dma = pltpu.SemaphoreType.DMA
    flops = 2 * tok * d_in * 3 * hd_all + 4 * nj * HD * (half + txt) * keys
    r1 = 2 * (2 * d_in // NDEV) // 128
    r2 = 2 * (4 * d_in // NDEV) // 128
    r1, r2 = -(-r1 // 8) * 8, -(-r2 // 8) * 8
    return pl.pallas_call(
        functools.partial(main_kernel, cfg, boff),
        out_shape=(jax.ShapeDtypeStruct((tok, hd_all), BF16), jax.ShapeDtypeStruct((nj, txt // 2, HD), BF16),
                   jax.ShapeDtypeStruct((NDEV, r2, 128), F32)),
        in_specs=[ANY, ANY, VM, ANY, ANY, ANY, ANY, VM, VM, VM, VM],
        out_specs=(ANY, VM, VM),
        scratch_shapes=[
            pltpu.VMEM((tok, d_in), BF16),
            pltpu.VMEM((tok, d_in), BF16),
            pltpu.VMEM((txt, d_in), BF16),
            pltpu.VMEM((nj * 4, 2 * tok, HD), BF16),
            pltpu.VMEM((nj * 4, HD, 2 * tok), BF16),
            pltpu.VMEM((nj * 4, 2 * tok, HD), BF16),
            pltpu.VMEM((nj, keys, HD), BF16),
            pltpu.VMEM((nj, HD, keys), BF16),
            pltpu.VMEM((nj, txt + half, HD), BF16),
            pltpu.VMEM((tok, 128), BF16),
            pltpu.VMEM((tok, 128), F32), pltpu.VMEM((tok, 128), F32), pltpu.VMEM((tok, 128), F32),
            pltpu.VMEM((2, d_in), F32), pltpu.VMEM((2, d_in), F32),
            pltpu.VMEM((NDEV, r1, 128), F32), pltpu.VMEM((r1, 128), F32), pltpu.VMEM((r2, 128), F32),
            dma((2,)), dma((3 * nj,)), dma((3, max(nj, 1))), dma((3,)), dma((3,)), dma((2, NDEV)), dma((2, NDEV)),
            dma((3, 3, nj, 4)), dma((3, 3, nj, 4)), dma((2, 3, nj)), dma((2, 3, nj)),
            dma((nj, 3, 4)), dma((nj, NCHIP, 2)),
        ],
        compiler_params=pltpu.CompilerParams(collective_id=1, has_side_effects=True, vmem_limit_bytes=VMEM_LIMIT),
        cost_estimate=pl.CostEstimate(flops=flops, bytes_accessed=2 * d_in * 3 * hd_all, transcendentals=0),
        name="attn",
    )(image, text, cond_vec, wm_img, wm_txt, w_img, w_txt, biases, gains, pos, omega)


def gelu(x):
    return x * (0.5 * (1.0 + jnp.tanh(0.7978845608028654 * (x + 0.044715 * (x * x * x)))))


def out_kernel(cfg, boff, o_hbm, x_hbm, xt_hbm, ot_ref, g2_ref, b_ref, wp_hbm, w1_hbm, w2_hbm, twp_hbm, tw1_hbm, tw2_hbm,
               out_ref, tout_ref, mi_ref, mt_ref,
               wa, wb, o, x, h, z, acc, a0, a1, o_t, x_t, h_t, z_t, a_t, part, rs, row,
               asem, bsem, lsem, ossem, orsem, pssem, prsem, rssem, rrsem, fssem, frsem):
    tok, txt, d, ff, s1, s2 = cfg
    me = lax.axis_index("cp")
    chip, core = me // 2, me % 2
    sib = chip * 2 + (1 - core)
    rows = txt // 2
    piece = rows // NCHIP
    nb = wa.shape[2]
    na = wa.shape[0]
    np_ = d // nb
    nf = ff // nb
    ft = ff // NCHIP
    nt = ft // nb
    nj = ot_ref.shape[0]

    def dev(c):
        return {"cp": c * 2 + core}

    off = pl.multiple_of(chip * ft, nb)
    segs_a = ((np_, wp_hbm, 0), (s1, w1_hbm, 0), (np_, twp_hbm, 0), (nt, tw1_hbm, off), (nf - s1, w1_hbm, s1 * nb))
    segs_b = ((s1, w2_hbm, 0), (nt, tw2_hbm, off), (nf - s1, w2_hbm, s1 * nb))

    def start(p, segs, is_a):
        lo = 0
        for n, ref, base in segs:
            @pl.when((p >= lo) & (p < lo + n))
            def _(lo=lo, ref=ref, base=base):
                sl = pl.ds(pl.multiple_of(base + (p - lo) * nb, nb), nb)
                slot = lax.rem(p, na)
                if is_a:
                    pltpu.make_async_copy(ref.at[:, sl], wa.at[slot], asem.at[slot]).start()
                else:
                    pltpu.make_async_copy(ref.at[sl, :], wb.at[slot], bsem.at[slot]).start()
            lo += n

    def get_a(p):
        start(p + na - 1, segs_a, True)
        slot = lax.rem(p, na)
        pltpu.make_async_copy(w1_hbm.at[:, 0:nb], wa.at[slot], asem.at[slot]).wait()
        return slot

    def get_b(p):
        start(p + na - 1, segs_b, False)
        slot = lax.rem(p, na)
        pltpu.make_async_copy(w2_hbm.at[0:nb, :], wb.at[slot], bsem.at[slot]).wait()
        return slot

    load_o = pltpu.make_async_copy(o_hbm, o, lsem.at[0])
    load_x = pltpu.make_async_copy(x_hbm, x, lsem.at[1])
    load_t = pltpu.make_async_copy(xt_hbm.at[pl.ds(pl.multiple_of(core * rows, 8), rows), :], x_t, lsem.at[2])
    load_o.start()
    start(jnp.int32(0), segs_a, True)
    load_x.start()
    for p in range(1, na - 1):
        start(jnp.int32(p), segs_a, True)
    for p in range(na - 1):
        start(jnp.int32(p), segs_b, False)
    load_t.start()

    barrier = pltpu.get_barrier_semaphore()
    for r in range(1, NCHIP):
        pl.semaphore_signal(barrier, inc=1, device_id=dev(lax.rem(chip + r, NCHIP)), device_id_type=MESH)
    pl.semaphore_signal(barrier, inc=1, device_id={"cp": sib}, device_id_type=MESH)
    pl.semaphore_wait(barrier, NCHIP)

    def o_copy(j, r, c_src, c_dst):
        return pltpu.make_async_remote_copy(
            src_ref=ot_ref.at[j], dst_ref=o_t.at[:, pl.ds(pl.multiple_of((j * NCHIP + c_src) * HD, HD), HD)],
            send_sem=ossem.at[j, r], recv_sem=orsem.at[j, r], device_id=dev(c_dst), device_id_type=MESH)

    for j in range(nj):
        for r in range(1, NCHIP):
            o_copy(j, r, chip, lax.rem(chip + r, NCHIP)).start()
        o_t[:, pl.ds(pl.multiple_of((j * NCHIP + chip) * HD, HD), HD)] = ot_ref[j]

    per = 4 * d // NDEV // 128
    for b, m in ((0, mi_ref), (1, mt_ref)):
        for dv in range(NDEV):
            for r in range(per):
                col = 2 * d + (dv * per + r) * 128
                brow = boff[b] + col // 128
                m[col // d:col // d + 1, col % d:col % d + 128] = g2_ref[dv, b * per + r:b * per + r + 1, :] + b_ref[brow:brow + 1, :]
    n128 = nb // 128

    load_o.wait()
    load_x.wait()

    def proj(p, carry):
        slot = get_a(p)
        sl = pl.ds(pl.multiple_of(p * nb, nb), nb)
        y = dot(o[...], wa[slot]) + bias_row(b_ref, boff[4] + p * n128, n128)
        h[:, sl] = x[:, sl].astype(F32) + mi_ref[2:3, sl] * y
        return carry
    lax.fori_loop(0, np_, proj, 0)

    def ln2(src, dst, m_ref, n):
        shift, scale = m_ref[3:4, :], 1.0 + m_ref[4:5, :]
        rb = 16

        def body(i, carry):
            r = pl.ds(pl.multiple_of(i * rb, rb), rb)
            dst[r, :] = ln_mod_rows(src[r, :], scale, shift).astype(BF16)
            return carry
        lax.fori_loop(0, n // rb, body, 0)

    ln2(h, z, mi_ref, tok)
    acc[...] = jnp.broadcast_to(bias_row(b_ref, boff[8], d // 128), acc.shape)

    def mlp(i, pa, pb, a_new, a_old):
        slot_b = get_b(pb)
        slot_a = get_a(pa)
        a_new[...] = gelu(dot(z[...], wa[slot_a]) + bias_row(b_ref, boff[6] + i * n128, n128)).astype(BF16)
        acc[...] += dot(a_old[...], wb[slot_b])

    def mlp_range(lo, hi, da, db):
        def two(k, carry):
            i = lo + 2 * k
            mlp(i, i + da, i - 1 + db, a1, a0)
            mlp(i + 1, i + 1 + da, i + db, a0, a1)
            return carry
        lax.fori_loop(0, (hi - lo) // 2, two, 0)

    slot = get_a(jnp.int32(np_))
    a0[...] = gelu(dot(z[...], wa[slot]) + bias_row(b_ref, boff[6], n128)).astype(BF16)
    mlp_range(1, s1, np_, 0)
    slot = get_b(jnp.int32(s1 - 1))
    acc[...] += dot(a0[...], wb[slot])

    load_t.wait()
    for j in range(nj):
        for r in range(1, NCHIP):
            o_copy(j, r, lax.rem(chip + NCHIP - r, NCHIP), chip).wait_recv()
    pa = np_ + s1

    def tproj(k, carry):
        slot = get_a(pa + k)
        sl = pl.ds(pl.multiple_of(k * nb, nb), nb)
        y = dot(o_t[...], wa[slot]) + bias_row(b_ref, boff[5] + k * n128, n128)
        h_t[:, sl] = x_t[:, sl].astype(F32) + mt_ref[2:3, sl] * y
        return carry
    lax.fori_loop(0, np_, tproj, 0)
    ln2(h_t, z_t, mt_ref, rows)

    for k in range(nt):
        slot = get_a(jnp.int32(pa + np_ + k))
        y = dot(z_t[...], wa[slot]) + bias_row(b_ref, boff[7] + (chip * nt + k) * n128, n128)
        a_t[:, k * nb:(k + 1) * nb] = gelu(y).astype(BF16)
    for k in range(nt):
        slot = get_b(jnp.int32(s1 + k))
        y = dot(a_t[:, k * nb:(k + 1) * nb], wb[slot])
        part[...] = y if k == 0 else part[...] + y

    def p_copy(r, c_src, c_dst):
        return pltpu.make_async_remote_copy(
            src_ref=part.at[pl.ds(pl.multiple_of(c_dst * piece, 8), piece), :], dst_ref=rs.at[c_src],
            send_sem=pssem.at[r], recv_sem=prsem.at[r], device_id=dev(c_dst), device_id_type=MESH)

    for r in range(1, NCHIP):
        p_copy(r, chip, lax.rem(chip + r, NCHIP)).start()
    mine = pl.ds(pl.multiple_of(chip * piece, 8), piece)
    rs[chip] = part[mine, :]

    da, db = np_ + np_ + nt, nt
    slot = get_a(jnp.int32(s1 + da))
    a0[...] = gelu(dot(z[...], wa[slot]) + bias_row(b_ref, boff[6] + s1 * n128, n128)).astype(BF16)
    mlp_range(s1 + 1, s2, da, db)

    for r in range(1, NCHIP):
        p_copy(r, lax.rem(chip + NCHIP - r, NCHIP), chip).wait_recv()
    tot = rs[0]
    for c in range(1, NCHIP):
        tot = tot + rs[c]
    y = h_t[mine, :] + mt_ref[5:6, :] * (tot + bias_row(b_ref, boff[9], d // 128))
    row[...] = y.astype(BF16)

    def r_copy(r, c_src, c_dst):
        return pltpu.make_async_remote_copy(
            src_ref=row, dst_ref=tout_ref.at[pl.ds(pl.multiple_of(core * rows + c_src * piece, 8), piece), :],
            send_sem=rssem.at[r], recv_sem=rrsem.at[r], device_id=dev(c_dst), device_id_type=MESH)

    for r in range(1, NCHIP):
        r_copy(r, chip, lax.rem(chip + r, NCHIP)).start()
    tout_ref[pl.ds(pl.multiple_of(core * rows + chip * piece, 8), piece), :] = row[...]

    mlp_range(s2, nf, da, db)

    for r in range(1, NCHIP):
        r_copy(r, lax.rem(chip + NCHIP - r, NCHIP), chip).wait_recv()
    ref = tout_ref.at[pl.ds(pl.multiple_of(core * rows, 8), rows), :]
    fwd = pltpu.make_async_remote_copy(src_ref=ref, dst_ref=ref, send_sem=fssem, recv_sem=frsem,
                                       device_id={"cp": sib}, device_id_type=MESH)
    fwd.start()

    slot = get_b(jnp.int32(nf - 1 + db))
    y = acc[...] + dot((a0 if (nf - 1 - s1) % 2 == 0 else a1)[...], wb[slot])
    out_ref[...] = (h[...] + mi_ref[5:6, :] * y).astype(BF16)

    fwd.wait()
    for j in range(nj):
        for r in range(1, NCHIP):
            o_copy(j, r, chip, lax.rem(chip + r, NCHIP)).wait_send()
    for r in range(1, NCHIP):
        c = lax.rem(chip + r, NCHIP)
        p_copy(r, chip, c).wait_send()
        r_copy(r, chip, c).wait_send()


def output(o_img, image, text, o_txt, g2, biases, boff, wp, w1, w2, twp, tw1, tw2):
    tok, d = image.shape
    txt = text.shape[0]
    ff = w1.shape[1]
    nb = 512
    nf = ff // nb
    s1 = 3 if nf > 8 else 1
    s2 = 18 if nf > 8 else 4
    na = 3
    rows = txt // 2
    ft = ff // NCHIP
    nj = o_txt.shape[0]
    dma = pltpu.SemaphoreType.DMA
    flops = 2 * tok * d * (d + 2 * ff) + 2 * rows * d * (d + 2 * ft)
    return pl.pallas_call(
        functools.partial(out_kernel, (tok, txt, d, ff, s1, s2), boff),
        out_shape=(jax.ShapeDtypeStruct((tok, d), BF16), jax.ShapeDtypeStruct((txt, d), BF16)),
        in_specs=[ANY, ANY, ANY, VM, VM, VM] + [ANY] * 6,
        out_specs=(VM, VM),
        scratch_shapes=[
            pltpu.VMEM((6, d), F32), pltpu.VMEM((6, d), F32),
            pltpu.VMEM((na, d, nb), BF16), pltpu.VMEM((na, nb, d), BF16),
            pltpu.VMEM((tok, d), BF16), pltpu.VMEM((tok, d), BF16), pltpu.VMEM((tok, d), F32), pltpu.VMEM((tok, d), BF16),
            pltpu.VMEM((tok, d), F32), pltpu.VMEM((tok, nb), BF16), pltpu.VMEM((tok, nb), BF16),
            pltpu.VMEM((rows, d), BF16), pltpu.VMEM((rows, d), BF16), pltpu.VMEM((rows, d), F32), pltpu.VMEM((rows, d), BF16),
            pltpu.VMEM((rows, ft), BF16), pltpu.VMEM((rows, d), F32), pltpu.VMEM((NCHIP, rows // NCHIP, d), F32),
            pltpu.VMEM((rows // NCHIP, d), BF16),
            dma((na,)), dma((na,)), dma((3,)), dma((nj, NCHIP)), dma((nj, NCHIP)), dma((NCHIP,)), dma((NCHIP,)),
            dma((NCHIP,)), dma((NCHIP,)), dma, dma,
        ],
        compiler_params=pltpu.CompilerParams(collective_id=2, has_side_effects=True, vmem_limit_bytes=VMEM_LIMIT),
        cost_estimate=pl.CostEstimate(flops=flops, bytes_accessed=2 * d * (d + 2 * ff), transcendentals=0),
        name="out",
    )(o_img, image, text, o_txt, g2, biases, wp, w1, w2, twp, tw1, tw2)


def rope_inputs(ids):
    d_t = HD // 8
    d_s = (HD - d_t) // 2
    widths = (d_t, d_s, d_s)
    n = ids.shape[0]
    pos = jnp.concatenate([jnp.broadcast_to(ids[:, a:a + 1], (n, w)) for a, w in enumerate(widths)], axis=1).astype(BF16)
    omega = jnp.concatenate([jnp.repeat(THETA ** (-jnp.arange(0, w, 2, dtype=F32) / w), 2) for w in widths])
    return pos, omega[None, :]


def device_fn(image, text, cond_vec, image_ids, *weights):
    (wm, bm, wqkv, bqkv, qg, kg, wp, bp, w1, b1, w2, b2) = weights[:12]
    (twm, tbm, twqkv, tbqkv, tqg, tkg, twp, tbp, tw1, tb1, tw2, tb2) = weights[12:]
    x, xt = image[0], text[0]
    parts = (bm, tbm, bqkv, tbqkv, bp, tbp, b1, tb1, b2, tb2)
    boff, rows = [], 0
    for b in parts:
        boff.append(rows)
        rows += b.shape[0] // 128
    biases = jnp.concatenate(parts).astype(F32).reshape(rows, 128)
    boff = tuple(boff)
    gains = jnp.stack([qg, kg, tqg, tkg]).astype(F32)
    pos, omega = rope_inputs(image_ids)
    o_img, o_txt, g2 = attention(x, xt, cond_vec, wm, twm, wqkv, twqkv, biases, boff, gains, pos, omega)
    image_out, text_out = output(o_img, x, xt, o_txt, g2, biases, boff, wp, w1, w2, twp, tw1, tw2)
    return image_out[None], text_out[None]


def solution(mesh):
    act = P("dp", "cp", None)
    txt = P("dp", None, None)
    in_specs = (act, txt, P("dp", None), P(("dp", "cp"), None)) + (P(),) * 24
    return jax.shard_map(device_fn, mesh=mesh, in_specs=in_specs, out_specs=(act, txt), check_vma=False)
```

time: 376 us -> 442 us (1.18)
  Pallas kernels: 348 us -> 418 us
  local copies, waits for them, and re-layouts: 18.9 us -> 13.8 us
    pallas_call x3 -> x2, Pallas kernels: 348 us -> 418 us  [the longest x1 313 us: attention(): pl.pallas_call(functools.partial(main_kernel, cfg, boff), out_shape=(jax....]
    broadcast_in_dim x10 -> x5, local copies, waits for them, and re-layouts: 10.8 us -> 0.48 us  [the longest x3 0.34 us: rope_inputs(): jnp.broadcast_to(ids[:, a:a + 1], (n, w))]
    unnamed x8 -> x11, local copies, waits for them, and re-layouts: 6.58 us -> 12.4 us
where the time goes in v3:
time: 442 us; the launch traced here: 437 us
  Pallas kernels  418 us (95%)
  local copies, waits for them, and re-layouts  13.8 us (3%)
    pallas_call x1, Pallas kernels, attention(): pl.pallas_call(functools.partial(main_kernel, cfg, boff), out_shape=(jax....  313 us
    pallas_call x1, Pallas kernels, output(): pl.pallas_call(functools.partial(out_kernel, (tok, txt, d, ff, s1, s2), b...  105 us
    unnamed x11, local copies, waits for them, and re-layouts  12.4 us

profile of v3, /device:TPU:0, one launch (start us, length us, event | category | flops | bytes accessed | tf_op | source)
XLA Modules:
  0.0 436.9 jit_solution(15557686537326454373)
XLA Ops:
  0.7 1.3 maximum_convert_fusion.g_ref
  2.0 0.8 convert_reduce_fusion.2
  2.8 0.1 broadcast_in_dim.45
  2.9 0.1 reshape.17
  2.9 0.1 broadcast_in_dim.46
  3.0 0.1 reshape.18
  3.1 0.6 maximum_bitcast_fusion.om_ref
  3.7 0.1 broadcast_in_dim.40
  3.9 0.1 broadcast_in_dim.44
  4.0 0.1 broadcast_in_dim.42
  4.1 0.8 pad_maximum_fusion.pos_ref
  4.9 0.8 constant_dynamic-update-slice_fusion.9
  5.6 0.8 constant_dynamic-update-slice_fusion.8
  6.4 0.7 constant_dynamic-update-slice_fusion.7
  7.1 0.7 constant_dynamic-update-slice_fusion.6
  7.9 0.7 constant_dynamic-update-slice_fusion.5
  8.6 0.7 constant_dynamic-update-slice_fusion.4
  9.3 0.7 constant_dynamic-update-slice_fusion.3
  10.0 0.7 constant_dynamic-update-slice_fusion.2
  10.7 0.7 constant_dynamic-update-slice_fusion.1
  11.4 0.7 constant_dynamic-update-slice_fusion
  12.1 0.8 bitcast_convert_fusion.b_ref
  12.9 312.6 %attn.1 = (bf16[384,3072]{1,0:T(8,128)(2,1)}, bf16[3,128,128]{2,1,0:T(8,128)(2,1)}, f32[16,16,128]{2,1,0:T(8,128)}) custom-call(bf16[384,3072]{1,0:T(8,128)(2,1)} %bitcast.13, bf16[256,3072]{1,0:T(8,128)(2,1)} %bitcast.15, bf16[1,3072]{1,0:T(2,128)(2,1)} %cond_ref.1, bf16[3072,18432]{1,0:T(8,128)(2,1)} %wmi_hbm.1, bf16[3072,18432]{1,0:T(8,128)(2,1)} %wmt_hbm.1, ...), custom_call_target="tpu_custom_call" | custom-call | flops 54458843136 | bytes 56623104 | tf_op jit(solution)/shard_map/attn/pallas_call | solution.py:504
  325.5 105.1 %out.1 = (bf16[384,3072]{1,0:T(8,128)(2,1)}, bf16[256,3072]{1,0:T(8,128)(2,1)}) custom-call(bf16[384,3072]{1,0:T(8,128)(2,1)} %get-tuple-element.7.o_hbm, bf16[384,3072]{1,0:T(8,128)(2,1)} %bitcast.14, bf16[256,3072]{1,0:T(8,128)(2,1)} %bitcast.16, bf16[3,128,128]{2,1,0:T(8,128)(2,1)} %get-tuple-element.8.ot_ref, f32[16,16,128]{2,1,0:T(8,128)} %get-tuple-element.9.g2_ref, ...), custom_call_target="tpu_custom_call" | custom-call | flops 70061654016 | bytes 169869312 | tf_op jit(solution)/shard_map/out/pallas_call | solution.py:762
  430.6 3.2 copy.41
  433.8 2.7 copy.42
  (2 shorter events, 0.0 us)

commit v4 on v2

v4 whole, which is shorter than its diff:
```python
import functools

import jax
import jax.numpy as jnp
import numpy as np
from jax import lax
from jax.experimental import pallas as pl
from jax.experimental.pallas import tpu as pltpu
from jax.sharding import PartitionSpec as P

EPS = 1e-6
THETA = 10000.0
F32 = jnp.float32
BF16 = jnp.bfloat16
HD = 128
NCHIP = 8
NDEV = 16
VM = pl.BlockSpec(memory_space=pltpu.VMEM)
ANY = pl.BlockSpec(memory_space=pl.ANY)
MESH = pl.DeviceIdType.MESH
VMEM_LIMIT = 67043328


def dot(a, b):
    return jnp.dot(a, b, preferred_element_type=F32)


def dot_t(a, b):
    return lax.dot_general(a, b, (((1,), (1,)), ((), ())), preferred_element_type=F32)


def lane_row(b_ref, start, n):
    return b_ref[pl.ds(start, n)].astype(F32).reshape(1, n)


def ln_mod_rows(x, scale1p, shift):
    xf = x.astype(F32)
    mean = jnp.mean(xf, axis=-1, keepdims=True)
    cent = xf - mean
    var = jnp.mean(cent * cent, axis=-1, keepdims=True)
    return scale1p * (cent * lax.rsqrt(var + EPS)) + shift


KINDS = (1, 2, 0)


def main_kernel(cfg, x_hbm, xt_hbm, cond_ref, wmi_hbm, wmt_hbm, wi_hbm, wt_hbm, bmi_ref, bmt_ref, bi_ref, bt_ref,
                qg_ref, kg_ref, tqg_ref, tkg_ref, pos_ref, om_ref,
                o_hbm, ot_ref, g2,
                w, xs, xm, xt, kn, kf, km, vn, vf, vm, qn, qf, qm, kb, vb, qb, posm, cos_t, se_t, so_t,
                mi, mt, g1, mine1, mine2, s0, s1, mx0, mx1, ost, otmp,
                xsem, wsem, msend, mrecv, gsend, grecv, ssem, rsem, fssem, frsem, ossem, orsem):
    tok, txt, d_in, heads, ck, mx = cfg
    nu = tok - mx
    hd_all = heads * HD
    nj = heads // NCHIP
    quad = 4
    wide = quad * HD
    half = tok * NCHIP
    me = lax.axis_index("cp")
    chip, core = me // 2, me % 2
    zh, cl = chip // quad, chip % quad
    sib = chip * 2 + (1 - core)
    mirror_chip = lax.rem(chip + quad, NCHIP)

    def dev(c):
        return {"cp": c * 2 + core}

    barrier = pltpu.get_barrier_semaphore()
    for r in range(1, NDEV):
        pl.semaphore_signal(barrier, inc=1, device_id={"cp": lax.rem(me + r, NDEV)}, device_id_type=MESH)
    load_x = pltpu.make_async_copy(x_hbm, xs, xsem.at[0])
    load_t = pltpu.make_async_copy(xt_hbm, xt, xsem.at[1])

    def x_copy():
        return pltpu.make_async_remote_copy(
            src_ref=x_hbm.at[pl.ds(nu, mx), :], dst_ref=xm, send_sem=msend.at[0], recv_sem=mrecv.at[0],
            device_id=dev(mirror_chip), device_id_type=MESH)

    def pos_copy():
        return pltpu.make_async_remote_copy(
            src_ref=pos_ref.at[pl.ds(nu, mx), :], dst_ref=posm, send_sem=msend.at[1], recv_sem=mrecv.at[1],
            device_id=dev(mirror_chip), device_id_type=MESH)

    mc = 2 * d_in // NDEV

    def tile_copy(what, a, b, slot):
        if what == "mod":
            ref = (wmi_hbm, wmt_hbm)[a]
            off = me * mc if b < 0 else 2 * d_in + me * 2 * mc + b * mc
            return [pltpu.make_async_copy(ref.at[:, pl.ds(pl.multiple_of(off, 128), mc)], w.at[slot, :, pl.ds(0, mc)], wsem.at[slot, 0])]
        if what == "txt":
            return [pltpu.make_async_copy(
                wt_hbm.at[:, pl.ds(pl.multiple_of(a * hd_all + (j * NCHIP + chip) * HD, HD), HD)],
                w.at[slot, :, pl.ds(j * HD, HD)], wsem.at[slot, j]) for j in range(nj)]
        kind, side = a
        off = kind * hd_all + b * NCHIP * HD + (zh if side == 0 else 1 - zh) * wide
        return [pltpu.make_async_copy(wi_hbm.at[:, pl.ds(pl.multiple_of(off, wide), wide)], w.at[slot], wsem.at[slot, 0])]

    def start(*a):
        for c in tile_copy(*a):
            c.start()

    def wait(*a):
        for c in tile_copy(*a):
            c.wait()
        return a[-1]

    def start_own(j, p):
        start("img", (KINDS[p // 2], p % 2), j, (2 + p) % 3)

    def start_txt(t):
        start("txt", KINDS[t], None, (2 + t) % 3)

    def start_mir(j, i):
        start("img", (KINDS[i], 0), j, (2 + i) % 3)

    def start_mod2(t):
        start("mod", t // 2, t % 2, (2 + t) % 3)

    start("mod", 0, -1, 0)
    start("mod", 1, -1, 1)
    load_x.start()
    load_t.start()

    c = cond_ref[...].astype(F32)
    act = (c * jax.nn.sigmoid(c)).astype(BF16)
    act = jnp.broadcast_to(act, (16, d_in))
    per = mc // 128

    def mod_rows(slot, buf, row):
        r = dot(act, w[slot, :, 0:mc])
        for i in range(per):
            buf[row + i:row + i + 1, :] = r[0:1, i * 128:(i + 1) * 128]

    def spread(buf, dst, k):
        return [pltpu.make_async_remote_copy(
            src_ref=buf, dst_ref=dst.at[me], send_sem=gsend.at[k, r], recv_sem=grecv.at[k, r],
            device_id={"cp": lax.rem(me + r, NDEV)}, device_id_type=MESH) for r in range(1, NDEV)]

    mine1[...] = jnp.zeros_like(mine1)
    start_own(0, 0)
    mod_rows(wait("mod", 0, -1, 0), mine1, 0)
    start_own(0, 1)
    mod_rows(wait("mod", 1, -1, 1), mine1, per)
    pl.semaphore_wait(barrier, NDEV - 1)
    gath1 = spread(mine1, g1, 0)
    for cp in gath1:
        cp.start()
    pos_copy().start()
    x_copy().start()
    g1[me] = mine1[...]

    def tables(pos, n):
        ang = pos.astype(F32) * om_ref[...]
        odd = lax.rem(lax.broadcasted_iota(jnp.int32, ang.shape, 1), 2) == 1
        sin = jnp.sin(ang)
        cos_t[0:n, :] = jnp.cos(ang)
        se_t[0:n, :] = jnp.where(odd, 0.0, -sin)
        so_t[0:n, :] = jnp.where(odd, sin, 0.0)

    tables(pos_ref[...], tok)
    for b_ref, m in ((bmi_ref, mi), (bmt_ref, mt)):
        for k in range(2):
            m[k:k + 1, :] = lane_row(b_ref, k * d_in, d_in)
    for cp in gath1:
        cp.wait()
    for b, m in ((0, mi), (1, mt)):
        for dv in range(NDEV):
            for r in range(per):
                col = (dv * per + r) * 128
                at = (slice(col // d_in, col // d_in + 1), slice(col % d_in, col % d_in + 128))
                m[at] = m[at] + g1[dv, b * per + r:b * per + r + 1, :]

    rb = 16

    def ln_rows(ref, m_ref, n):
        shift = m_ref[0:1, :]
        scale = 1.0 + m_ref[1:2, :]

        def body(i, carry):
            sl = pl.ds(pl.multiple_of(i * rb, rb), rb)
            ref[sl, :] = ln_mod_rows(ref[sl, :], scale, shift).astype(BF16)
            return carry
        lax.fori_loop(0, n // rb, body, 0)

    def norm_rope(y, gain, rope):
        ms = jnp.mean(y * y, axis=-1, keepdims=True)
        y = y * lax.rsqrt(ms + EPS) * gain
        if rope:
            n = y.shape[0]
            y = y * cos_t[0:n, :] + pltpu.roll(y, HD - 1, 1) * se_t[0:n, :] + pltpu.roll(y, 1, 1) * so_t[0:n, :]
        return y

    def place(kind, s_chip, row, n, j):
        if kind == 0:
            return qb.at[j, pl.ds(pl.multiple_of(txt + s_chip * tok + row, 128), n)]
        at = pl.multiple_of(txt + core * half + s_chip * tok + row, 128)
        return kb.at[j, pl.ds(at, n)] if kind == 1 else vb.at[j, :, pl.ds(at, n)]

    def qkv_copy(kind, ty, j, src_cl, src_zh, dst_cl, idx):
        buf = ((qn, qf, qm), (kn, kf, km), (vn, vf, vm))[kind][ty]
        n = (tok, nu, mx)[ty]
        s_chip = src_zh * quad + src_cl
        tgt = (1 - src_zh if ty == 1 else src_zh) * quad + dst_cl
        if ty == 2:
            dst = place(kind, lax.rem(s_chip + quad, NCHIP), nu, n, j)
        else:
            dst = place(kind, s_chip, 0, n, j)
        return pltpu.make_async_remote_copy(
            src_ref=buf.at[j * quad + dst_cl], dst_ref=dst, send_sem=ssem.at[kind, ty, j, idx[0]],
            recv_sem=rsem.at[kind, ty, j, idx[1]], device_id=dev(tgt), device_id_type=MESH)

    def out_copies(kind, ty, j):
        if ty == 1:
            return [qkv_copy(kind, 1, j, cl, zh, c, (c, cl)) for c in range(quad)]
        return [qkv_copy(kind, ty, j, cl, zh, lax.rem(cl + r, quad), (r, r)) for r in range(1, quad)]

    def in_copies(kind, ty, j):
        if ty == 1:
            return [qkv_copy(kind, 1, j, c, 1 - zh, cl, (c, c)) for c in range(quad)]
        return [qkv_copy(kind, ty, j, lax.rem(cl + quad - r, quad), zh, cl, (r, r)) for r in range(1, quad)]

    def own_copy(kind, ty, j):
        buf = ((qn, qf, qm), (kn, kf, km), (vn, vf, vm))[kind][ty]
        n = (tok, nu, mx)[ty]
        dst = place(kind, mirror_chip, nu, n, j) if ty == 2 else place(kind, chip, 0, n, j)
        dst[...] = buf[j * quad + cl]

    def make(kind, ty, j, slot):
        src = xm if ty == 2 else xs
        n = (tok, nu, mx)[ty]
        buf = ((qn, qf, qm), (kn, kf, km), (vn, vf, vm))[kind][ty]

        def cols(p, carry):
            col = pl.multiple_of(p * 2 * HD, 2 * HD)
            boff = kind * hd_all + j * NCHIP * HD + (1 - zh if ty == 1 else zh) * wide + col
            y2 = dot(src[0:n, :], w[slot, :, pl.ds(col, 2 * HD)]) + lane_row(bi_ref, pl.multiple_of(boff, 256), 2 * HD)
            for hh in range(2):
                y = y2[:, hh * HD:(hh + 1) * HD]
                if kind == 2:
                    buf[j * quad + 2 * p + hh] = y.T.astype(BF16)
                else:
                    gain = (qg_ref, kg_ref)[kind][...].astype(F32).reshape(1, HD)
                    buf[j * quad + 2 * p + hh] = norm_rope(y, gain, True).astype(BF16)
            return carry
        lax.fori_loop(0, 2, cols, 0)

    load_x.wait()
    ln_rows(xs, mi, tok)

    def own_pass(j, carry):
        for p in range(6):
            kind, side = KINDS[p // 2], p % 2
            if p + 2 < 6:
                start_own(j, p + 2)
            else:
                @pl.when(j < nj - 1)
                def _():
                    start_own(j + 1, p - 4)

                @pl.when(j == nj - 1)
                def _():
                    start_txt(p - 4)
            slot = wait("img", (kind, side), j, (2 + p) % 3)
            make(kind, side, j, slot)
            for cp in out_copies(kind, side, j):
                cp.start()
            if side == 0:
                own_copy(kind, 0, j)
        return carry
    lax.fori_loop(0, nj, own_pass, 0)

    load_t.wait()
    ln_rows(xt, mt, txt)
    for t, kind in enumerate(KINDS):
        if t == 0:
            start_txt(2)
        else:
            start_mir(0, t - 1)
        slot = wait("txt", kind, None, (2 + t) % 3)
        y3 = dot(xt[...], w[slot, :, 0:nj * HD])
        for j in range(nj):
            pair0 = kind * hd_all + (j * NCHIP + chip - lax.rem(chip, 2)) * HD
            b2 = lane_row(bt_ref, pl.multiple_of(pair0, 256), 2 * HD)
            y = y3[:, j * HD:(j + 1) * HD] + jnp.where(lax.rem(chip, 2) == 0, b2[:, 0:HD], b2[:, HD:2 * HD])
            if kind == 2:
                vb[j, :, 0:txt] = y.T.astype(BF16)
            else:
                gain = (tqg_ref, tkg_ref)[kind][...].astype(F32).reshape(1, HD)
                (qb, kb)[kind][j, 0:txt] = norm_rope(y, gain, False).astype(BF16)

    pos_copy().wait_recv()
    tables(posm[...], mx)
    x_copy().wait_recv()
    ln_rows(xm, mi, mx)

    def mir_pass(j, carry):
        for i, kind in enumerate(KINDS):
            if i == 0:
                start_mir(j, 2)
            else:
                @pl.when(j < nj - 1)
                def _():
                    start_mir(j + 1, i - 1)

                @pl.when(j == nj - 1)
                def _():
                    start_mod2(i - 1)
            slot = wait("img", (kind, 0), j, (2 + i) % 3)
            make(kind, 2, j, slot)
            for cp in out_copies(kind, 2, j):
                cp.start()
            own_copy(kind, 2, j)
        return carry
    lax.fori_loop(0, nj, mir_pass, 0)

    mine2[...] = jnp.zeros_like(mine2)
    for t in range(4):
        if t + 2 < 4:
            start_mod2(t + 2)
        mod_rows(wait("mod", t // 2, t % 2, (2 + t) % 3), mine2, t * per)
    gath2 = spread(mine2, g2, 1)
    for cp in gath2:
        cp.start()
    g2[me] = mine2[...]

    scale2 = (HD ** -0.5) * 1.4426950408889634
    keys = txt + 2 * half
    nchunk = keys // ck
    qt = 256
    ntile = (txt + half) // qt
    group = 2 * tok // qt
    ngroup = NCHIP // 2

    def to_sibling(kind, j):
        ref = (kb.at[j, pl.ds(pl.multiple_of(txt + core * half, 128), half)] if kind == 1
               else vb.at[j, :, pl.ds(pl.multiple_of(txt + core * half, 128), half)])
        return pltpu.make_async_remote_copy(
            src_ref=ref, dst_ref=ref, send_sem=fssem.at[kind - 1, j], recv_sem=frsem.at[kind - 1, j],
            device_id={"cp": sib}, device_id_type=MESH)

    def collect(j):
        for kind in KINDS:
            for ty in range(3):
                for cp in in_copies(kind, ty, j):
                    cp.wait_recv()
            if kind != 0:
                to_sibling(kind, j).start()

    def tile_start(t):
        g = (t - 1) // group
        plane = lax.rem(chip // 2 + 1 + g, ngroup)
        row = txt + plane * (2 * tok) + lax.rem(t - 1, group) * qt
        return pl.multiple_of(jnp.where(t == 0, 0, row), 128)

    def qk(j, q, i, s_ref, mxv):
        sl = pl.ds(pl.multiple_of(i * ck, ck), ck)
        s = dot_t(kb[j, sl], q)
        s_ref[sl, :] = s
        return jnp.maximum(mxv, jnp.max(s.reshape(ck // 8, 8, qt), axis=0))

    def sm(j, i, s_ref, m, lsum, acc):
        sl = pl.ds(pl.multiple_of(i * ck, ck), ck)
        p = jnp.exp2((s_ref[sl, :] - m) * scale2)
        lsum = lsum + jnp.sum(p.reshape(ck // 8, 8, qt), axis=0)
        acc = acc + dot(vb[j, :, sl], p.astype(BF16))
        return lsum, acc

    def new_max():
        return jnp.full((8, qt), -jnp.inf, F32)

    def o_remote(j, c_src, c_dst):
        src = ost.at[j, pl.ds(pl.multiple_of(c_dst * tok, 128), tok)]
        dst = o_hbm.at[:, pl.ds(pl.multiple_of((j * NCHIP + c_src) * HD, HD), HD)]
        return pltpu.make_async_remote_copy(
            src_ref=src, dst_ref=dst, send_sem=ossem.at[j, c_dst], recv_sem=orsem.at[j, c_src],
            device_id=dev(c_dst), device_id_type=MESH)

    def o_local(j):
        src = ost.at[j, pl.ds(pl.multiple_of(chip * tok, 128), tok)]
        dst = o_hbm.at[:, pl.ds(pl.multiple_of((j * NCHIP + chip) * HD, HD), HD)]
        return pltpu.make_async_copy(src, dst, ossem.at[j, chip])

    def o_send(j, g):
        plane = lax.rem(chip // 2 + 1 + g, ngroup)
        for y in range(2):
            c = plane * 2 + y

            @pl.when(c != chip)
            def _():
                o_remote(j, chip, c).start()

            @pl.when(c == chip)
            def _():
                o_local(j).start()

    def finish(j, t, lsum, acc):
        tot = jnp.sum(lsum, axis=0, keepdims=True)
        o = (acc / tot).T.astype(BF16)

        @pl.when(t == 0)
        def _():
            otmp[...] = o
            ot_ref[j] = otmp[pl.ds(pl.multiple_of(core * (txt // 2), 8), txt // 2), :]

        @pl.when(t > 0)
        def _():
            ost[j, pl.ds(pl.multiple_of(tile_start(t) - txt, 128), qt)] = o

            @pl.when(lax.rem(t, group) == 0)
            def _():
                o_send(j, t // group - 1)

    def pair(j, t, s_cur, mx_cur, s_nxt, mx_nxt, has_next):
        m = jnp.max(mx_cur[...], axis=0, keepdims=True)
        lsum = jnp.zeros((8, qt), F32)
        acc = jnp.zeros((HD, qt), F32)
        if has_next:
            q = qb[j, pl.ds(tile_start(t + 1), qt)]

            def body(i, carry):
                lsum, acc, mxv = carry
                mxv = qk(j, q, i, s_nxt, mxv)
                lsum, acc = sm(j, i, s_cur, m, lsum, acc)
                return lsum, acc, mxv
            lsum, acc, mxv = lax.fori_loop(0, nchunk, body, (lsum, acc, new_max()))
            mx_nxt[...] = mxv
        else:
            def body(i, carry):
                return sm(j, i, s_cur, m, *carry)
            lsum, acc = lax.fori_loop(0, nchunk, body, (lsum, acc))
        finish(j, t, lsum, acc)

    collect(0)

    def head(j, carry):
        for kind in (1, 2):
            to_sibling(kind, j).wait()
        q = qb[j, 0:qt]

        def first(i, mxv):
            return qk(j, q, i, s0, mxv)
        mx0[...] = lax.fori_loop(0, nchunk, first, new_max())

        def two(i, carry):
            pair(j, 2 * i, s0, mx0, s1, mx1, True)
            pair(j, 2 * i + 1, s1, mx1, s0, mx0, True)
            return carry
        lax.fori_loop(0, (ntile - 1) // 2, two, 0)
        if nj > 1:
            @pl.when(j < nj - 1)
            def _():
                collect(j + 1)
        pair(j, jnp.int32(ntile - 1), s0, mx0, s1, mx1, False)
        return carry
    lax.fori_loop(0, nj, head, 0)

    for cp in gath2:
        cp.wait()
    x_copy().wait_send()
    pos_copy().wait_send()

    def drain(j, carry):
        for kind in KINDS:
            for ty in range(3):
                for cp in out_copies(kind, ty, j):
                    cp.wait_send()
        o_local(j).wait()
        for r in range(1, NCHIP):
            c = lax.rem(chip + r, NCHIP)
            o_remote(j, chip, c).wait_send()
            o_remote(j, c, chip).wait_recv()
        return carry
    lax.fori_loop(0, nj, drain, 0)


def attention(image, text, cond_vec, wm_img, wm_txt, w_img, w_txt, flat, pos, omega):
    tok, d_in = image.shape
    txt = text.shape[0]
    hd_all = w_img.shape[1] // 3
    heads = hd_all // HD
    nj = heads // NCHIP
    half = tok * NCHIP
    keys = txt + 2 * half
    ck = 1280
    mx = 128
    nu = tok - mx
    cfg = (tok, txt, d_in, heads, ck, mx)
    dma = pltpu.SemaphoreType.DMA
    flops = 2 * tok * d_in * 3 * hd_all + 4 * nj * HD * (half + txt) * keys
    per = 2 * d_in // NDEV // 128
    r1, r2 = -(-2 * per // 8) * 8, -(-4 * per // 8) * 8
    row_sets = [pltpu.VMEM((nj * 4, n, HD), BF16) for n in (tok, nu, mx)]
    col_sets = [pltpu.VMEM((nj * 4, HD, n), BF16) for n in (tok, nu, mx)]
    table = pltpu.VMEM((tok, 128), F32)
    return pl.pallas_call(
        functools.partial(main_kernel, cfg),
        out_shape=(jax.ShapeDtypeStruct((tok, hd_all), BF16), jax.ShapeDtypeStruct((nj, txt // 2, HD), BF16),
                   jax.ShapeDtypeStruct((NDEV, r2, 128), F32)),
        in_specs=[ANY, ANY, VM, ANY, ANY, ANY, ANY] + [VM] * 10,
        out_specs=(ANY, VM, VM),
        scratch_shapes=[
            pltpu.VMEM((3, d_in, 4 * HD), BF16),
            pltpu.VMEM((tok, d_in), BF16), pltpu.VMEM((mx, d_in), BF16), pltpu.VMEM((txt, d_in), BF16),
            *row_sets, *col_sets, *row_sets,
            pltpu.VMEM((nj, keys, HD), BF16), pltpu.VMEM((nj, HD, keys), BF16), pltpu.VMEM((nj, txt + half, HD), BF16),
            pltpu.VMEM((mx, 128), BF16), table, table, table,
            pltpu.VMEM((2, d_in), F32), pltpu.VMEM((2, d_in), F32),
            pltpu.VMEM((NDEV, r1, 128), F32), pltpu.VMEM((r1, 128), F32), pltpu.VMEM((r2, 128), F32),
            pltpu.VMEM((keys, 256), F32), pltpu.VMEM((keys, 256), F32), pltpu.VMEM((8, 256), F32), pltpu.VMEM((8, 256), F32),
            pltpu.VMEM((nj, half, HD), BF16), pltpu.VMEM((txt, HD), BF16),
            dma((2,)), dma((3, max(nj, 1))), dma((2,)), dma((2,)), dma((2, NDEV)), dma((2, NDEV)),
            dma((3, 3, nj, 4)), dma((3, 3, nj, 4)), dma((2, nj)), dma((2, nj)), dma((nj, NCHIP)), dma((nj, NCHIP)),
        ],
        compiler_params=pltpu.CompilerParams(collective_id=1, has_side_effects=True, vmem_limit_bytes=VMEM_LIMIT),
        cost_estimate=pl.CostEstimate(flops=flops, bytes_accessed=3 * d_in * 3 * hd_all, transcendentals=0),
        name="attn",
    )(image, text, cond_vec, wm_img, wm_txt, w_img, w_txt, *flat, pos, omega)


def gelu(x):
    return x * (0.5 * (1.0 + jnp.tanh(0.7978845608028654 * (x + 0.044715 * (x * x * x)))))


def out_kernel(cfg, o_hbm, x_hbm, xt_hbm, ot_ref, g2_ref, bmi_ref, bmt_ref, bp_ref, tbp_ref, b1_ref, tb1_ref, b2_ref, tb2_ref, wp_hbm, w1_hbm, w2_hbm, twp_hbm, tw1_hbm, tw2_hbm,
               out_ref, tout_ref, mi_ref, mt_ref,
               wa, wb, o, x, h, z, acc, a0, a1, o_t, x_t, h_t, z_t, a_t, part, rs, row,
               asem, bsem, lsem, ossem, orsem, pssem, prsem, rssem, rrsem, fssem, frsem):
    tok, txt, d, ff, s1, s2 = cfg
    me = lax.axis_index("cp")
    chip, core = me // 2, me % 2
    sib = chip * 2 + (1 - core)
    rows = txt // 2
    piece = rows // NCHIP
    nb = wa.shape[2]
    na = wa.shape[0]
    np_ = d // nb
    nf = ff // nb
    ft = ff // NCHIP
    nt = ft // nb
    nj = ot_ref.shape[0]

    def dev(c):
        return {"cp": c * 2 + core}

    off = pl.multiple_of(chip * ft, nb)
    segs_a = ((np_, wp_hbm, 0), (s1, w1_hbm, 0), (np_, twp_hbm, 0), (nt, tw1_hbm, off), (nf - s1, w1_hbm, s1 * nb))
    segs_b = ((s1, w2_hbm, 0), (nt, tw2_hbm, off), (nf - s1, w2_hbm, s1 * nb))

    def start(p, segs, is_a):
        lo = 0
        for n, ref, base in segs:
            @pl.when((p >= lo) & (p < lo + n))
            def _(lo=lo, ref=ref, base=base):
                sl = pl.ds(pl.multiple_of(base + (p - lo) * nb, nb), nb)
                slot = lax.rem(p, na)
                if is_a:
                    pltpu.make_async_copy(ref.at[:, sl], wa.at[slot], asem.at[slot]).start()
                else:
                    pltpu.make_async_copy(ref.at[sl, :], wb.at[slot], bsem.at[slot]).start()
            lo += n

    def get_a(p):
        start(p + na - 1, segs_a, True)
        slot = lax.rem(p, na)
        pltpu.make_async_copy(w1_hbm.at[:, 0:nb], wa.at[slot], asem.at[slot]).wait()
        return slot

    def get_b(p):
        start(p + na - 1, segs_b, False)
        slot = lax.rem(p, na)
        pltpu.make_async_copy(w2_hbm.at[0:nb, :], wb.at[slot], bsem.at[slot]).wait()
        return slot

    load_o = pltpu.make_async_copy(o_hbm, o, lsem.at[0])
    load_x = pltpu.make_async_copy(x_hbm, x, lsem.at[1])
    load_t = pltpu.make_async_copy(xt_hbm.at[pl.ds(pl.multiple_of(core * rows, 8), rows), :], x_t, lsem.at[2])
    load_o.start()
    start(jnp.int32(0), segs_a, True)
    load_x.start()
    for p in range(1, na - 1):
        start(jnp.int32(p), segs_a, True)
    for p in range(na - 1):
        start(jnp.int32(p), segs_b, False)
    load_t.start()

    barrier = pltpu.get_barrier_semaphore()
    for r in range(1, NCHIP):
        pl.semaphore_signal(barrier, inc=1, device_id=dev(lax.rem(chip + r, NCHIP)), device_id_type=MESH)
    pl.semaphore_signal(barrier, inc=1, device_id={"cp": sib}, device_id_type=MESH)
    pl.semaphore_wait(barrier, NCHIP)

    def o_copy(j, r, c_src, c_dst):
        return pltpu.make_async_remote_copy(
            src_ref=ot_ref.at[j], dst_ref=o_t.at[:, pl.ds(pl.multiple_of((j * NCHIP + c_src) * HD, HD), HD)],
            send_sem=ossem.at[j, r], recv_sem=orsem.at[j, r], device_id=dev(c_dst), device_id_type=MESH)

    for j in range(nj):
        for r in range(1, NCHIP):
            o_copy(j, r, chip, lax.rem(chip + r, NCHIP)).start()
        o_t[:, pl.ds(pl.multiple_of((j * NCHIP + chip) * HD, HD), HD)] = ot_ref[j]

    per = 4 * d // NDEV // 128
    for b, (b_ref, m) in enumerate(((bmi_ref, mi_ref), (bmt_ref, mt_ref))):
        for k in range(2, 6):
            m[k:k + 1, :] = lane_row(b_ref, k * d, d)
        for dv in range(NDEV):
            for r in range(per):
                col = 2 * d + (dv * per + r) * 128
                at = (slice(col // d, col // d + 1), slice(col % d, col % d + 128))
                m[at] = m[at] + g2_ref[dv, b * per + r:b * per + r + 1, :]

    load_o.wait()
    load_x.wait()

    def proj(p, carry):
        slot = get_a(p)
        sl = pl.ds(pl.multiple_of(p * nb, nb), nb)
        y = dot(o[...], wa[slot]) + lane_row(bp_ref, pl.multiple_of(p * nb, nb), nb)
        h[:, sl] = x[:, sl].astype(F32) + mi_ref[2:3, sl] * y
        return carry
    lax.fori_loop(0, np_, proj, 0)

    def ln2(src, dst, m_ref, n):
        shift, scale = m_ref[3:4, :], 1.0 + m_ref[4:5, :]
        rb = 16

        def body(i, carry):
            r = pl.ds(pl.multiple_of(i * rb, rb), rb)
            dst[r, :] = ln_mod_rows(src[r, :], scale, shift).astype(BF16)
            return carry
        lax.fori_loop(0, n // rb, body, 0)

    ln2(h, z, mi_ref, tok)
    acc[...] = jnp.broadcast_to(lane_row(b2_ref, 0, d), acc.shape)

    def mlp(i, pa, pb, a_new, a_old):
        slot_b = get_b(pb)
        slot_a = get_a(pa)
        a_new[...] = gelu(dot(z[...], wa[slot_a]) + lane_row(b1_ref, pl.multiple_of(i * nb, nb), nb)).astype(BF16)
        acc[...] += dot(a_old[...], wb[slot_b])

    def mlp_range(lo, hi, da, db):
        def two(k, carry):
            i = lo + 2 * k
            mlp(i, i + da, i - 1 + db, a1, a0)
            mlp(i + 1, i + 1 + da, i + db, a0, a1)
            return carry
        lax.fori_loop(0, (hi - lo) // 2, two, 0)

    slot = get_a(jnp.int32(np_))
    a0[...] = gelu(dot(z[...], wa[slot]) + lane_row(b1_ref, 0, nb)).astype(BF16)
    mlp_range(1, s1, np_, 0)
    slot = get_b(jnp.int32(s1 - 1))
    acc[...] += dot(a0[...], wb[slot])

    load_t.wait()
    for j in range(nj):
        for r in range(1, NCHIP):
            o_copy(j, r, lax.rem(chip + NCHIP - r, NCHIP), chip).wait_recv()
    pa = np_ + s1

    def tproj(k, carry):
        slot = get_a(pa + k)
        sl = pl.ds(pl.multiple_of(k * nb, nb), nb)
        y = dot(o_t[...], wa[slot]) + lane_row(tbp_ref, pl.multiple_of(k * nb, nb), nb)
        h_t[:, sl] = x_t[:, sl].astype(F32) + mt_ref[2:3, sl] * y
        return carry
    lax.fori_loop(0, np_, tproj, 0)
    ln2(h_t, z_t, mt_ref, rows)

    for k in range(nt):
        slot = get_a(jnp.int32(pa + np_ + k))
        y = dot(z_t[...], wa[slot]) + lane_row(tb1_ref, pl.multiple_of(off + k * nb, nb), nb)
        a_t[:, k * nb:(k + 1) * nb] = gelu(y).astype(BF16)
    for k in range(nt):
        slot = get_b(jnp.int32(s1 + k))
        y = dot(a_t[:, k * nb:(k + 1) * nb], wb[slot])
        part[...] = y if k == 0 else part[...] + y

    def p_copy(r, c_src, c_dst):
        return pltpu.make_async_remote_copy(
            src_ref=part.at[pl.ds(pl.multiple_of(c_dst * piece, 8), piece), :], dst_ref=rs.at[c_src],
            send_sem=pssem.at[r], recv_sem=prsem.at[r], device_id=dev(c_dst), device_id_type=MESH)

    for r in range(1, NCHIP):
        p_copy(r, chip, lax.rem(chip + r, NCHIP)).start()
    mine = pl.ds(pl.multiple_of(chip * piece, 8), piece)
    rs[chip] = part[mine, :]

    da, db = np_ + np_ + nt, nt
    slot = get_a(jnp.int32(s1 + da))
    a0[...] = gelu(dot(z[...], wa[slot]) + lane_row(b1_ref, s1 * nb, nb)).astype(BF16)
    mlp_range(s1 + 1, s2, da, db)

    for r in range(1, NCHIP):
        p_copy(r, lax.rem(chip + NCHIP - r, NCHIP), chip).wait_recv()
    tot = rs[0]
    for c in range(1, NCHIP):
        tot = tot + rs[c]
    y = h_t[mine, :] + mt_ref[5:6, :] * (tot + lane_row(tb2_ref, 0, d))
    row[...] = y.astype(BF16)

    def r_copy(r, c_src, c_dst):
        return pltpu.make_async_remote_copy(
            src_ref=row, dst_ref=tout_ref.at[pl.ds(pl.multiple_of(core * rows + c_src * piece, 8), piece), :],
            send_sem=rssem.at[r], recv_sem=rrsem.at[r], device_id=dev(c_dst), device_id_type=MESH)

    for r in range(1, NCHIP):
        r_copy(r, chip, lax.rem(chip + r, NCHIP)).start()
    tout_ref[pl.ds(pl.multiple_of(core * rows + chip * piece, 8), piece), :] = row[...]

    mlp_range(s2, nf, da, db)

    for r in range(1, NCHIP):
        r_copy(r, lax.rem(chip + NCHIP - r, NCHIP), chip).wait_recv()
    ref = tout_ref.at[pl.ds(pl.multiple_of(core * rows, 8), rows), :]
    fwd = pltpu.make_async_remote_copy(src_ref=ref, dst_ref=ref, send_sem=fssem, recv_sem=frsem,
                                       device_id={"cp": sib}, device_id_type=MESH)
    fwd.start()

    slot = get_b(jnp.int32(nf - 1 + db))
    y = acc[...] + dot((a0 if (nf - 1 - s1) % 2 == 0 else a1)[...], wb[slot])
    out_ref[...] = (h[...] + mi_ref[5:6, :] * y).astype(BF16)

    fwd.wait()
    for j in range(nj):
        for r in range(1, NCHIP):
            o_copy(j, r, chip, lax.rem(chip + r, NCHIP)).wait_send()
    for r in range(1, NCHIP):
        c = lax.rem(chip + r, NCHIP)
        p_copy(r, chip, c).wait_send()
        r_copy(r, chip, c).wait_send()


def output(o_img, image, text, o_txt, g2, flat, wp, w1, w2, twp, tw1, tw2):
    tok, d = image.shape
    txt = text.shape[0]
    ff = w1.shape[1]
    nb = 512
    nf = ff // nb
    s1 = 3 if nf > 8 else 1
    s2 = 18 if nf > 8 else 4
    na = 3
    rows = txt // 2
    ft = ff // NCHIP
    nj = o_txt.shape[0]
    dma = pltpu.SemaphoreType.DMA
    flops = 2 * tok * d * (d + 2 * ff) + 2 * rows * d * (d + 2 * ft)
    return pl.pallas_call(
        functools.partial(out_kernel, (tok, txt, d, ff, s1, s2)),
        out_shape=(jax.ShapeDtypeStruct((tok, d), BF16), jax.ShapeDtypeStruct((txt, d), BF16)),
        in_specs=[ANY, ANY, ANY, VM, VM] + [VM] * 8 + [ANY] * 6,
        out_specs=(VM, VM),
        scratch_shapes=[
            pltpu.VMEM((6, d), F32), pltpu.VMEM((6, d), F32),
            pltpu.VMEM((na, d, nb), BF16), pltpu.VMEM((na, nb, d), BF16),
            pltpu.VMEM((tok, d), BF16), pltpu.VMEM((tok, d), BF16), pltpu.VMEM((tok, d), F32), pltpu.VMEM((tok, d), BF16),
            pltpu.VMEM((tok, d), F32), pltpu.VMEM((tok, nb), BF16), pltpu.VMEM((tok, nb), BF16),
            pltpu.VMEM((rows, d), BF16), pltpu.VMEM((rows, d), BF16), pltpu.VMEM((rows, d), F32), pltpu.VMEM((rows, d), BF16),
            pltpu.VMEM((rows, ft), BF16), pltpu.VMEM((rows, d), F32), pltpu.VMEM((NCHIP, rows // NCHIP, d), F32),
            pltpu.VMEM((rows // NCHIP, d), BF16),
            dma((na,)), dma((na,)), dma((3,)), dma((nj, NCHIP)), dma((nj, NCHIP)), dma((NCHIP,)), dma((NCHIP,)),
            dma((NCHIP,)), dma((NCHIP,)), dma, dma,
        ],
        compiler_params=pltpu.CompilerParams(collective_id=2, has_side_effects=True, vmem_limit_bytes=VMEM_LIMIT),
        cost_estimate=pl.CostEstimate(flops=flops, bytes_accessed=2 * d * (d + 2 * ff), transcendentals=0),
        name="out",
    )(o_img, image, text, o_txt, g2, *flat, wp, w1, w2, twp, tw1, tw2)


def rope_inputs(ids):
    d_t = HD // 8
    d_s = (HD - d_t) // 2
    widths = (d_t, d_s, d_s)
    lane = lax.broadcasted_iota(jnp.int32, (1, HD), 1)
    pos = jnp.where(lane < d_t, ids[:, 0:1], jnp.where(lane < d_t + d_s, ids[:, 1:2], ids[:, 2:3])).astype(BF16)
    omega = np.concatenate([np.repeat(THETA ** (-np.arange(0, w, 2, dtype=np.float32) / np.float32(w)), 2) for w in widths])
    return pos, jnp.asarray(omega.astype(np.float32)[None, :])


def device_fn(image, text, cond_vec, image_ids, *weights):
    (wm, bm, wqkv, bqkv, qg, kg, wp, bp, w1, b1, w2, b2) = weights[:12]
    (twm, tbm, twqkv, tbqkv, tqg, tkg, twp, tbp, tw1, tb1, tw2, tb2) = weights[12:]
    x, xt = image[0], text[0]
    pos, omega = rope_inputs(image_ids)
    o_img, o_txt, g2 = attention(x, xt, cond_vec, wm, twm, wqkv, twqkv, (bm, tbm, bqkv, tbqkv, qg, kg, tqg, tkg), pos, omega)
    image_out, text_out = output(o_img, x, xt, o_txt, g2, (bm, tbm, bp, tbp, b1, tb1, b2, tb2), wp, w1, w2, twp, tw1, tw2)
    return image_out[None], text_out[None]


def solution(mesh):
    act = P("dp", "cp", None)
    txt = P("dp", None, None)
    in_specs = (act, txt, P("dp", None), P(("dp", "cp"), None)) + (P(),) * 24
    return jax.shard_map(device_fn, mesh=mesh, in_specs=in_specs, out_specs=(act, txt), check_vma=False)
```

time: 376 us -> 356 us (0.947)
  local copies, waits for them, and re-layouts: 18.9 us -> 6.7 us
    pallas_call x1, Pallas kernels: 224 us -> 241 us  [attention(): pl.pallas_call(functools.partial(main_kernel, cfg), out_shape=(jax.ShapeD...]
    pallas_call x1 -> x0, Pallas kernels: 14.5 us -> none  [modulation(): pl.pallas_call(mod_kernel, out_shape=jax.ShapeDtypeStruct((NDEV, pad, 128...]
    broadcast_in_dim x10 -> x0, local copies, waits for them, and re-layouts: 10.8 us -> none  [the longest x8 10.6 us: device_fn(): row = lambda v: v[None, :]]
    pallas_call x1, Pallas kernels: 110 us -> 106 us  [output(): pl.pallas_call(functools.partial(out_kernel, (tok, txt, d, ff, s1, s2)),...]
where the time goes in v4:
time: 356 us; the launch traced here: 355 us
  Pallas kernels  347 us (97%)
  local copies, waits for them, and re-layouts  6.7 us (2%)
    pallas_call x1, Pallas kernels, attention(): pl.pallas_call(functools.partial(main_kernel, cfg), out_shape=(jax.ShapeD...  241 us
    pallas_call x1, Pallas kernels, output(): pl.pallas_call(functools.partial(out_kernel, (tok, txt, d, ff, s1, s2)),...  106 us

profile of v4, /device:TPU:0, one launch (start us, length us, event | category | flops | bytes accessed | tf_op | source)
XLA Modules:
  0.0 355.3 jit_solution(13252874588686941776)
XLA Ops:
  0.6 0.8 slice_reduce_fusion.2
  1.5 0.9 select_convert_fusion.pos_ref
  2.3 241.5 %attn.1 = (bf16[384,3072]{1,0:T(8,128)(2,1)}, bf16[3,128,128]{2,1,0:T(8,128)(2,1)}, f32[16,16,128]{2,1,0:T(8,128)}) custom-call(bf16[384,3072]{1,0:T(8,128)(2,1)} %bitcast.4, bf16[256,3072]{1,0:T(8,128)(2,1)} %bitcast.6, bf16[1,3072]{1,0:T(2,128)(2,1)} %cond_ref.1, bf16[3072,18432]{1,0:T(8,128)(2,1)} %wmi_hbm.1, bf16[3072,18432]{1,0:T(8,128)(2,1)} %wmt_hbm.1, ...), custom_call_target="tpu_custom_call" | custom-call | flops 54458843136 | bytes 84934656 | tf_op jit(solution)/shard_map/attn/pallas_call | solution.py:497
  243.8 105.6 %out.1 = (bf16[384,3072]{1,0:T(8,128)(2,1)}, bf16[256,3072]{1,0:T(8,128)(2,1)}) custom-call(bf16[384,3072]{1,0:T(8,128)(2,1)} %get-tuple-element.7.o_hbm, bf16[384,3072]{1,0:T(8,128)(2,1)} %bitcast.5, bf16[256,3072]{1,0:T(8,128)(2,1)} %bitcast.7, bf16[3,128,128]{2,1,0:T(8,128)(2,1)} %get-tuple-element.8.ot_ref, f32[16,16,128]{2,1,0:T(8,128)} %get-tuple-element.9.g2_ref, ...), custom_call_target="tpu_custom_call" | custom-call | flops 70061654016 | bytes 169869312 | tf_op jit(solution)/shard_map/out/pallas_call | solution.py:751
  349.4 3.2 copy.33
  352.6 2.7 copy.34
  (1 shorter events, 0.0 us)
